TPU v7x, 32 devices: a whole 2x2x4 slice. The times are simulated.
32 devices in a mesh: gx: 8 (over z, y), gy: 4 (over x, core).
Axes of the slice: x: 2, y: 2, z: 4, core: 2. Of those that a mesh axis runs over, the one named last changes fastest.
Arguments:
- fine_nodes: bfloat16 [32768, 512], P(('gx', 'gy')), may hold values from -6 to 6
- edge_latent: bfloat16 [196608, 512], P(('gx', 'gy')), may hold values from -6 to 6
- boundary: int32 [4096], P(('gx', 'gy')), may hold values from 0 to 1023, as said below
- fine_src: int32 [196608], P(('gx', 'gy')), may hold values from 0 to 2175, as said below
- fine_dst: int32 [196608], P(('gx', 'gy')), may hold values from 0 to 1023
- parent_one: int32 [32768], P(('gx', 'gy')), may hold values from 0 to 831, as said below
- weight_one: bfloat16 [32768], P(('gx', 'gy')), may hold values from 0.049804688 to 0.29882812
- coarse_src_one: int32 [49152], P(('gx', 'gy')), may hold values from 0 to 831, as said below
- coarse_dst_one: int32 [49152], P(('gx', 'gy')), may hold values from 0 to 255
- parent_two: int32 [8192], P(('gx', 'gy')), may hold values from 0 to 351, as said below
- weight_two: bfloat16 [8192], P(('gx', 'gy')), may hold values from 0.099609375 to 0.5
- coarse_src_two: int32 [12288], P(('gx', 'gy')), may hold values from 0 to 351, as said below
- coarse_dst_two: int32 [12288], P(('gx', 'gy')), may hold values from 0 to 63
- fine_message_in: bfloat16 [1536, 512], replicated, may hold values from -0.15625 to 0.15625
- fine_message_out: bfloat16 [512, 512], replicated, may hold values from -0.25 to 0.25
- fine_message_gain: bfloat16 [512], replicated, may hold values from 0.25 to 1.75
- fine_update_in: bfloat16 [1024, 512], replicated, may hold values from -0.1875 to 0.1875
- fine_update_out: bfloat16 [512, 512], replicated, may hold values from -0.25 to 0.25
- fine_update_gain: bfloat16 [512], replicated, may hold values from 0.25 to 1.75
- coarse_message_in: bfloat16 [1024, 512], replicated, may hold values from -0.1875 to 0.1875
- coarse_message_out: bfloat16 [512, 512], replicated, may hold values from -0.25 to 0.25
- coarse_message_gain: bfloat16 [512], replicated, may hold values from 0.25 to 1.75
- coarse_update_in: bfloat16 [1024, 512], replicated, may hold values from -0.1875 to 0.1875
- coarse_update_out: bfloat16 [512, 512], replicated, may hold values from -0.25 to 0.25
- coarse_update_gain: bfloat16 [512], replicated, may hold values from 0.25 to 1.75
Outputs:
- fine_out: bfloat16 [32768, 512], P(('gx', 'gy'))
Inputs may be any that keep to these rules, and one draw needn't show every extreme that they name: `boundary`: each device's 128 entries are distinct local row numbers of its own fine nodes. `fine_src`: an entry below 1024 is a local row of the edge's own device; an entry 1024 + k * 128 + r names boundary row r of the device at grid offset (k // 3 - 1, k % 3 - 1) along (gx, gy), with wrap; k is never 4. `parent_one`: an entry below 256 is a first coarse level row of the fine node's own device; an entry 256 + k * 64 + r names rim row r of the device at grid offset (k // 3 - 1, k % 3 - 1) along (gx, gy), with wrap; k is never 4. `coarse_src_one`: an entry below 256 is a first coarse level row of the edge's own device; an entry 256 + k * 64 + r names rim row r of the device at grid offset (k // 3 - 1, k % 3 - 1) along (gx, gy), with wrap; k is never 4. `parent_two`: an entry below 64 is a second coarse level row of the node's own device; an entry 64 + k * 32 + r names rim row r of the device at grid offset (k // 3 - 1, k % 3 - 1) along (gx, gy), with wrap; k is never 4. `coarse_src_two`: an entry below 64 is a second coarse level row of the edge's own device; an entry 64 + k * 32 + r names rim row r of the device at grid offset (k // 3 - 1, k % 3 - 1) along (gx, gy), with wrap; k is never 4.
All inputs are finite; a program needn't handle non-finite values.
Results may differ from a plain program's by a relative error of at most 0.012.
Values may be sent and summed in bfloat16 or wider, within the bound.
No kernel may reach another device: no remote copies, remote signals or barrier semaphores. Data moves between devices by JAX's collectives and lax.ppermute only.
A program may use at most 128 MiB of HBM per device.

v0:
```python
import jax
import jax.numpy as jnp
from jax import lax
from jax.sharding import PartitionSpec as P

NC1_DEV = 256
NC2_DEV = 64
CB1 = 64
CB2 = 32


def padded(cells, sides, width):
    for axis, dim in sides:
        count = lax.axis_size(axis)
        head = lax.slice_in_dim(cells, 0, width, axis=dim)
        tail = lax.slice_in_dim(cells, cells.shape[dim] - width, cells.shape[dim], axis=dim)
        cells = jnp.concatenate(
            [
                lax.ppermute(tail, axis, [(i, (i + 1) % count) for i in range(count)]),
                cells,
                lax.ppermute(head, axis, [((i + 1) % count, i) for i in range(count)]),
            ],
            axis=dim,
        )
    return cells


def passed_along(value, axis, steps):
    count = lax.axis_size(axis)
    pairs = [(source, (source + steps) % count) for source in range(count)]
    return lax.ppermute(value, axis, pairs)


def normed(preact, scales):
    average = jnp.mean(preact, axis=-1, keepdims=True)
    centred = preact - average
    spread = jnp.mean(centred * centred, axis=-1, keepdims=True)
    return centred * lax.rsqrt(spread + 1e-05) * scales.astype(jnp.float32)


def finish(preact, project_out, scales):
    hidden = jax.nn.silu(preact).astype(jnp.bfloat16)
    return normed(jnp.dot(hidden, project_out, preferred_element_type=jnp.float32), scales)


def summed(targets, messages, node_count):
    onehot = (lax.iota(jnp.int32, node_count)[:, None] == targets[None, :]).astype(jnp.bfloat16)
    return jnp.dot(onehot, messages, preferred_element_type=jnp.float32)


def node_update(states, incoming, update_in, update_out, update_gain):
    features = states.shape[1]
    preact = jnp.dot(states, update_in[:features], preferred_element_type=jnp.float32)
    preact = preact + jnp.dot(
        incoming.astype(jnp.bfloat16), update_in[features:], preferred_element_type=jnp.float32
    )
    return (states.astype(jnp.float32) + finish(preact, update_out, update_gain)).astype(
        jnp.bfloat16
    )


def extend_rows(owned_rows, rim_count):
    rims = padded(owned_rows[:rim_count][None, None], (("gx", 0), ("gy", 1)), 1)
    return jnp.concatenate([owned_rows, rims.reshape(-1, owned_rows.shape[1])], axis=0)


def lift_rows(coarse_rows, rim_count, parents):
    rims = padded(coarse_rows[:rim_count][None, None], (("gx", 0), ("gy", 1)), 1)
    extended = jnp.concatenate([coarse_rows, rims.reshape(-1, coarse_rows.shape[1])], axis=0)
    return jnp.take(extended, parents, axis=0).astype(jnp.float32)


def coarse_level(
    owned_rows,
    extended,
    sources,
    targets,
    message_in,
    message_out,
    message_gain,
    update_in,
    update_out,
    update_gain,
):
    features = owned_rows.shape[1]
    source_proj = jnp.dot(extended, message_in[:features], preferred_element_type=jnp.float32)
    target_proj = jnp.dot(owned_rows, message_in[features:], preferred_element_type=jnp.float32)
    preact = jnp.take(source_proj, sources, axis=0) + jnp.take(target_proj, targets, axis=0)
    messages = finish(preact, message_out, message_gain).astype(jnp.bfloat16)
    incoming = summed(targets, messages, owned_rows.shape[0])
    return node_update(owned_rows, incoming, update_in, update_out, update_gain)


def restrict(states, parents, weights, local_count, rim_count):
    features = states.shape[1]
    positions = lax.iota(jnp.int32, local_count + 9 * rim_count)
    spread_matrix = jnp.where(
        positions[:, None] == parents[None, :], weights[None, :], jnp.zeros((), jnp.bfloat16)
    )
    spread_sums = jnp.dot(spread_matrix, states, preferred_element_type=jnp.float32)
    blocks = spread_sums[local_count:].reshape(3, 3, rim_count, features)
    column = blocks[1]
    for step_x in (-1, 1):
        column = column + passed_along(
            blocks[step_x + 1].astype(jnp.bfloat16), "gx", step_x
        ).astype(jnp.float32)
    inbound = column[1]
    for step_y in (-1, 1):
        inbound = inbound + passed_along(
            column[step_y + 1].astype(jnp.bfloat16), "gy", step_y
        ).astype(jnp.float32)
    owned = jnp.concatenate(
        [spread_sums[:rim_count] + inbound, spread_sums[rim_count:local_count]], axis=0
    )
    return owned.astype(jnp.bfloat16)


def per_device(
    fine_nodes,
    edge_latent,
    boundary,
    fine_src,
    fine_dst,
    parent_one,
    weight_one,
    coarse_src_one,
    coarse_dst_one,
    parent_two,
    weight_two,
    coarse_src_two,
    coarse_dst_two,
    fine_message_in,
    fine_message_out,
    fine_message_gain,
    fine_update_in,
    fine_update_out,
    fine_update_gain,
    coarse_message_in,
    coarse_message_out,
    coarse_message_gain,
    coarse_update_in,
    coarse_update_out,
    coarse_update_gain,
):
    features = fine_nodes.shape[1]
    edge_rows = jnp.take(fine_nodes, boundary, axis=0)
    beside_all = padded(edge_rows[None, None], (("gx", 0), ("gy", 1)), 1)
    source_weights = fine_message_in[:features]
    own_proj = jnp.dot(fine_nodes, source_weights, preferred_element_type=jnp.float32)
    target_proj = jnp.dot(
        fine_nodes, fine_message_in[features : 2 * features], preferred_element_type=jnp.float32
    )
    latent_proj = jnp.dot(
        edge_latent, fine_message_in[2 * features :], preferred_element_type=jnp.float32
    )
    around_proj = jnp.dot(
        beside_all.reshape(-1, features), source_weights, preferred_element_type=jnp.float32
    )
    source_proj = jnp.concatenate([own_proj, around_proj], axis=0)
    preact = (
        jnp.take(source_proj, fine_src, axis=0)
        + jnp.take(target_proj, fine_dst, axis=0)
        + latent_proj
    )
    messages = finish(preact, fine_message_out, fine_message_gain).astype(jnp.bfloat16)
    incoming = summed(fine_dst, messages, fine_nodes.shape[0])
    fine_new = node_update(fine_nodes, incoming, fine_update_in, fine_update_out, fine_update_gain)
    level_one = restrict(fine_new, parent_one, weight_one, NC1_DEV, CB1)
    level_one_new = coarse_level(
        level_one,
        extend_rows(level_one, CB1),
        coarse_src_one,
        coarse_dst_one,
        coarse_message_in,
        coarse_message_out,
        coarse_message_gain,
        coarse_update_in,
        coarse_update_out,
        coarse_update_gain,
    )
    level_two = restrict(level_one_new, parent_two, weight_two, NC2_DEV, CB2)
    level_two_new = coarse_level(
        level_two,
        extend_rows(level_two, CB2),
        coarse_src_two,
        coarse_dst_two,
        coarse_message_in,
        coarse_message_out,
        coarse_message_gain,
        coarse_update_in,
        coarse_update_out,
        coarse_update_gain,
    )
    level_one_final = (
        level_one_new.astype(jnp.float32) + lift_rows(level_two_new, CB2, parent_two)
    ).astype(jnp.bfloat16)
    return (fine_new.astype(jnp.float32) + lift_rows(level_one_final, CB1, parent_one)).astype(
        jnp.bfloat16
    )


def solution(mesh):
    in_specs = (
        P(("gx", "gy"), None),
        P(("gx", "gy"), None),
        P(("gx", "gy")),
        P(("gx", "gy")),
        P(("gx", "gy")),
        P(("gx", "gy")),
        P(("gx", "gy")),
        P(("gx", "gy")),
        P(("gx", "gy")),
        P(("gx", "gy")),
        P(("gx", "gy")),
        P(("gx", "gy")),
        P(("gx", "gy")),
        P(),
        P(),
        P(),
        P(),
        P(),
        P(),
        P(),
        P(),
        P(),
        P(),
        P(),
        P(),
    )
    out_specs = P(("gx", "gy"), None)
    return jax.shard_map(
        per_device, mesh=mesh, in_specs=in_specs, out_specs=out_specs, check_vma=False
    )
```

profile of v0, /device:TPU:1, one launch (start us, length us, event | category | flops | bytes accessed | tf_op | source)
XLA Modules:
  0.0 254.1 jit_solution(3212110500046166699)
XLA Ops:
  5.9 3.1 %collective-permute-start.1 = (bf16[1,1,128,512]{3,2,1,0:T(8,128)(2,1)S(1)}, bf16[1,1,128,512]{3,2,1,0:T(8,128)(2,1)S(1)}, u32[]{:S(2)}, u32[]{:S(2)}) collective-permute-start(bf16[1,1,128,512]{3,2,1,0:T(8,128)(2,1)S(1)} %bitcast_select_fusion), channel_id=1, source_target_pairs={{4,0},{8,4},{12,8},{16,12},{20,16},{24,20},{28,24},{0,28},{5,1},{9... | collective-permute-start | bytes 393224 | tf_op jit(solution)/shard_map/ppermute | solution.py:21
  9.0 3.4 %fusion.53 = f32[1024,512]{1,0:T(8,128)} fusion(bf16[1024,512]{1,0:T(8,128)(2,1)} %param.25, bf16[1536,512]{1,0:T(8,128)(2,1)} %param.38), kind=kOutput, calls=%fused_computation.87 | convolution fusion | flops 536870912 | bytes 3670016 | tf_op jit(solution)/shard_map/dot_general | solution.py:149
  19.5 24.7 %gather_fusion.2 = f32[6144,512]{1,0:T(8,128)} fusion(f32[1024,512]{1,0:T(8,128)S(1)} %fusion.34, s32[6144]{0:T(1024)S(1)} %fusion.86), kind=kCustom, calls=%fused_computation.2 | custom fusion | bytes 25190400 | tf_op jit(solution)/shard_map/jit(_take)/gather | solution.py:162
  49.1 6.1 %collective-permute-done.2 = bf16[3,1,128,512]{3,2,1,0:T(8,128)(2,1)S(1)} collective-permute-done((bf16[3,1,128,512]{3,2,1,0:T(8,128)(2,1)S(1)}, bf16[3,1,128,512]{3,2,1,0:T(8,128)(2,1)S(1)}, u32[]{:S(2)}, u32[]{:S(2)}) %collective-permute-start.2) | collective-permute-done | bytes 393248 | tf_op jit(solution)/shard_map/ppermute | solution.py:19
  61.2 28.8 %gather_fusion.1 = f32[6144,512]{1,0:T(8,128)} fusion(f32[2176,512]{1,0:T(8,128)} %pad_maximum_fusion, s32[6144]{0:T(1024)S(1)} %fusion.85), kind=kCustom, calls=%fused_computation.1 | custom fusion | bytes 25190400 | tf_op jit(solution)/shard_map/jit(_take)/gather | solution.py:161
  90.0 20.9 %fusion.106 = (f32[6144]{0:T(1024)S(1)}, f32[6144,512]{0,1:T(8,128)}) fusion(bf16[512,512]{1,0:T(8,128)(2,1)S(1)} %copy-done, f32[6144,512]{1,0:T(8,128)} %gather_fusion.2, f32[6144,512]{1,0:T(8,128)} %gather_fusion.1, bf16[6144,512]{1,0:T(8,128)(2,1)} %param.26, pred[6144]{0:T(1024)(128)(4,1)S(1)} %get-tuple-element.34, ...), kind=kOutput, calls=%fused_computation.195 | convolution fusion | flops 6473902080 | bytes 45125632 | tf_op jit(solution)/shard_map/dot_general | solution.py:43
  110.9 6.1 %multiply_reduce_fusion = f32[6144]{0:T(1024)S(1)} fusion(f32[6144,512]{0,1:T(8,128)} %get-tuple-element.19, f32[6144]{0:T(1024)S(1)} %broadcast_multiply_fusion), kind=kLoop, calls=%fused_computation.12 | loop fusion | flops 9431040 | bytes 12632064 | tf_op jit(solution)/shard_map/reduce_sum | solution.py:37
  117.0 15.6 %multiply_convert_fusion.5 = bf16[1024,512]{1,0:T(8,128)(2,1)} fusion(f32[1024,512]{1,0:T(8,128)S(1)} %fusion.36, f32[6144,512]{0,1:T(8,128)} %get-tuple-element.19, f32[512]{0:T(512)S(1)} %convert_element_type.149, f32[6144]{0:T(1024)S(1)} %add_rsqrt_fusion, f32[6144]{0:T(1024)S(1)} %broadcast_multiply_fusion, s32[6144]{0:T(1024)S(1)} %copy-done.16, ...), kind=kOutput, calls=%fused_computation.32 | convolution fusion | flops 7001866240 | bytes 16328704 | tf_op jit(solution)/shard_map/dot_general | solution.py:54
  139.0 4.4 %collective-permute-done.4 = bf16[3,64,512]{2,1,0:T(8,128)(2,1)S(1)} collective-permute-done((bf16[3,64,512]{2,1,0:T(8,128)(2,1)S(1)}, bf16[3,64,512]{2,1,0:T(8,128)(2,1)S(1)}, u32[]{:S(2)}, u32[]{:S(2)}) %collective-permute-start.4) | collective-permute-done | bytes 196640 | tf_op jit(solution)/shard_map/ppermute | solution.py:31
  143.4 4.2 %collective-permute-done.5 = bf16[3,64,512]{2,1,0:T(8,128)(2,1)S(1)} collective-permute-done((bf16[3,64,512]{2,1,0:T(8,128)(2,1)S(1)}, bf16[3,64,512]{2,1,0:T(8,128)(2,1)S(1)}, u32[]{:S(2)}, u32[]{:S(2)}) %collective-permute-start.5) | collective-permute-done | bytes 196640 | tf_op jit(solution)/shard_map/ppermute | solution.py:31
  152.1 4.1 %collective-permute-start.9 = (bf16[1,1,64,512]{3,2,1,0:T(8,128)(2,1)S(1)}, bf16[1,1,64,512]{3,2,1,0:T(8,128)(2,1)S(1)}, u32[]{:S(2)}, u32[]{:S(2)}) collective-permute-start(bf16[1,1,64,512]{3,2,1,0:T(8,128)(2,1)S(1)} %bitcast.65), channel_id=1, source_target_pairs={{4,0},{8,4},{12,8},{16,12},{20,16},{24,20},{28,24},{0,28},{5,1},{9... | collective-permute-start | bytes 196616 | tf_op jit(solution)/shard_map/ppermute | solution.py:21
  156.6 5.0 %gather_fusion.4 = f32[1536,512]{1,0:T(8,128)} fusion(f32[256,512]{1,0:T(8,128)S(1)} %fusion.42, s32[2048]{0:T(1024)S(1)} %pad_clamp_fusion), kind=kCustom, calls=%fused_computation.4 | custom fusion | bytes 6297600 | tf_op jit(solution)/shard_map/jit(_take)/gather | solution.py:88
  164.2 3.2 %collective-permute-done.10 = bf16[3,1,64,512]{3,2,1,0:T(8,128)(2,1)S(1)} collective-permute-done((bf16[3,1,64,512]{3,2,1,0:T(8,128)(2,1)S(1)}, bf16[3,1,64,512]{3,2,1,0:T(8,128)(2,1)S(1)}, u32[]{:S(2)}, u32[]{:S(2)}) %collective-permute-start.10) | collective-permute-done | bytes 196640 | tf_op jit(solution)/shard_map/ppermute | solution.py:19
  170.4 5.0 %gather_fusion.3 = f32[1536,512]{1,0:T(8,128)} fusion(f32[832,512]{1,0:T(8,128)S(1)} %fusion.21, s32[2048]{0:T(1024)S(1)} %pad_clamp_fusion.1), kind=kCustom, calls=%fused_computation.3 | custom fusion | bytes 6297600 | tf_op jit(solution)/shard_map/jit(_take)/gather | solution.py:88
  175.3 4.9 %fusion.111 = (f32[1536]{0:T(1024)S(1)}, f32[1536,512]{0,1:T(8,128)S(1)}) fusion(bf16[512,512]{1,0:T(8,128)(2,1)} %param.45, f32[1536,512]{1,0:T(8,128)} %gather_fusion.4, f32[1536,512]{1,0:T(8,128)} %gather_fusion.3, pred[1536]{0:T(1024)(128)(4,1)S(1)} %copy-done.31, pred[1536]{0:T(1024)(128)(4,1)S(1)} %copy-done.32), kind=kOutput, calls=%fused_computation.198 | convolution fusion | flops 812382720 | bytes 9970688 | tf_op jit(solution)/shard_map/dot_general | solution.py:43
  182.4 3.1 %multiply_convert_fusion.18 = bf16[256,512]{1,0:T(8,128)(2,1)S(1)} fusion(f32[256,512]{1,0:T(8,128)S(1)} %fusion.49, f32[1536,512]{0,1:T(8,128)} %copy-done.6, f32[512]{0:T(512)S(1)} %copy-done.33, f32[1536]{0:T(1024)S(1)} %add_rsqrt_fusion.1, f32[1536]{0:T(1024)S(1)} %broadcast_multiply_fusion.1, s32[1536]{0:T(1024)S(1)} %copy-done.19, ...), kind=kOutput, calls=%fused_computation.65 | convolution fusion | flops 541327360 | bytes 4476928 | tf_op jit(solution)/shard_map/dot_general | solution.py:54
  188.2 2.9 %collective-permute-done.12 = bf16[3,32,512]{2,1,0:T(8,128)(2,1)S(1)} collective-permute-done((bf16[3,32,512]{2,1,0:T(8,128)(2,1)S(1)}, bf16[3,32,512]{2,1,0:T(8,128)(2,1)S(1)}, u32[]{:S(2)}, u32[]{:S(2)}) %collective-permute-start.12) | collective-permute-done | bytes 98336 | tf_op jit(solution)/shard_map/ppermute | solution.py:31
  191.1 4.4 %collective-permute-done.13 = bf16[3,32,512]{2,1,0:T(8,128)(2,1)S(1)} collective-permute-done((bf16[3,32,512]{2,1,0:T(8,128)(2,1)S(1)}, bf16[3,32,512]{2,1,0:T(8,128)(2,1)S(1)}, u32[]{:S(2)}, u32[]{:S(2)}) %collective-permute-start.13) | collective-permute-done | bytes 98336 | tf_op jit(solution)/shard_map/ppermute | solution.py:31
  199.1 4.1 %collective-permute-start.17 = (bf16[1,1,32,512]{3,2,1,0:T(8,128)(2,1)S(1)}, bf16[1,1,32,512]{3,2,1,0:T(8,128)(2,1)S(1)}, u32[]{:S(2)}, u32[]{:S(2)}) collective-permute-start(bf16[1,1,32,512]{3,2,1,0:T(8,128)(2,1)S(1)} %bitcast.72), channel_id=1, source_target_pairs={{4,0},{8,4},{12,8},{16,12},{20,16},{24,20},{28,24},{0,28},{5,1},{9... | collective-permute-start | bytes 98312 | tf_op jit(solution)/shard_map/ppermute | solution.py:21
  204.5 2.9 %collective-permute-start.18 = (bf16[3,1,32,512]{3,2,1,0:T(8,128)(2,1)S(1)}, bf16[3,1,32,512]{3,2,1,0:T(8,128)(2,1)S(1)}, u32[]{:S(2)}, u32[]{:S(2)}) collective-permute-start(bf16[3,1,32,512]{3,2,1,0:T(8,128)(2,1)S(1)} %pad_maximum_fusion.12), channel_id=1, source_target_pairs={{0,1},{1,2},{2,3},{3,0},{4,5},{5,6},{6,7},{7,4},{8,9},{9,10},{10,1... | collective-permute-start | bytes 294920 | tf_op jit(solution)/shard_map/ppermute | solution.py:19
  220.0 4.8 %collective-permute-start.21 = (bf16[1,1,32,512]{3,2,1,0:T(8,128)(2,1)S(1)}, bf16[1,1,32,512]{3,2,1,0:T(8,128)(2,1)S(1)}, u32[]{:S(2)}, u32[]{:S(2)}) collective-permute-start(bf16[1,1,32,512]{3,2,1,0:T(8,128)(2,1)S(1)} %slice_bitcast_fusion.5), channel_id=1, source_target_pairs={{4,0},{8,4},{12,8},{16,12},{20,16},{24,20},{28,24},{0,28},{5,1},{9... | collective-permute-start | bytes 98312 | tf_op jit(solution)/shard_map/ppermute | solution.py:21
  233.0 4.8 %collective-permute-start.25 = (bf16[1,1,64,512]{3,2,1,0:T(8,128)(2,1)S(1)}, bf16[1,1,64,512]{3,2,1,0:T(8,128)(2,1)S(1)}, u32[]{:S(2)}, u32[]{:S(2)}) collective-permute-start(bf16[1,1,64,512]{3,2,1,0:T(8,128)(2,1)S(1)} %slice_bitcast_fusion.1), channel_id=1, source_target_pairs={{4,0},{8,4},{12,8},{16,12},{20,16},{24,20},{28,24},{0,28},{5,1},{9... | collective-permute-start | bytes 196616 | tf_op jit(solution)/shard_map/ppermute | solution.py:21
  240.7 3.5 %collective-permute-done.26 = bf16[3,1,64,512]{3,2,1,0:T(8,128)(2,1)S(1)} collective-permute-done((bf16[3,1,64,512]{3,2,1,0:T(8,128)(2,1)S(1)}, bf16[3,1,64,512]{3,2,1,0:T(8,128)(2,1)S(1)}, u32[]{:S(2)}, u32[]{:S(2)}) %collective-permute-start.26) | collective-permute-done | bytes 196640 | tf_op jit(solution)/shard_map/ppermute | solution.py:19
  246.5 4.0 %gather_fusion.8 = bf16[1024,512]{1,0:T(8,128)(2,1)S(1)} fusion(bf16[832,512]{1,0:T(8,128)(2,1)S(1)} %pad_maximum_fusion.2, s32[1024]{0:T(1024)S(1)} %fusion.87), kind=kCustom, calls=%fused_computation.8 | custom fusion | bytes 2101248 | tf_op jit(solution)/shard_map/jit(_take)/gather | solution.py:70
  (224 shorter events, 79.1 us)
Async XLA Ops:
  3.8 41.0 %collective-permute-start = (bf16[1,1,128,512]{3,2,1,0:T(8,128)(2,1)S(1)}, bf16[1,1,128,512]{3,2,1,0:T(8,128)(2,1)S(1)}, u32[]{:S(2)}, u32[]{:S(2)}) collective-permute-start(bf16[1,1,128,512]{3,2,1,0:T(8,128)(2,1)S(1)} %bitcast_select_fusion), channel_id=1, source_target_pairs={{0,4},{4,8},{8,12},{12,16},{16,20},{20,24},{24,28},{28,0},{1,5},{5... | collective-permute-start | bytes 393224 | tf_op jit(solution)/shard_map/ppermute | solution.py:19
  5.9 38.9 %collective-permute-start.1 = (bf16[1,1,128,512]{3,2,1,0:T(8,128)(2,1)S(1)}, bf16[1,1,128,512]{3,2,1,0:T(8,128)(2,1)S(1)}, u32[]{:S(2)}, u32[]{:S(2)}) collective-permute-start(bf16[1,1,128,512]{3,2,1,0:T(8,128)(2,1)S(1)} %bitcast_select_fusion), channel_id=1, source_target_pairs={{4,0},{8,4},{12,8},{16,12},{20,16},{24,20},{28,24},{0,28},{5,1},{9... | collective-permute-start | bytes 393224 | tf_op jit(solution)/shard_map/ppermute | solution.py:21
  44.8 10.4 %collective-permute-start.2 = (bf16[3,1,128,512]{3,2,1,0:T(8,128)(2,1)S(1)}, bf16[3,1,128,512]{3,2,1,0:T(8,128)(2,1)S(1)}, u32[]{:S(2)}, u32[]{:S(2)}) collective-permute-start(bf16[3,1,128,512]{3,2,1,0:T(8,128)(2,1)S(1)} %pad_maximum_fusion.5), channel_id=1, source_target_pairs={{0,1},{1,2},{2,3},{3,0},{4,5},{5,6},{6,7},{7,4},{8,9},{9,10},{10,1... | collective-permute-start | bytes 1179656 | tf_op jit(solution)/shard_map/ppermute | solution.py:19
  47.0 9.5 %collective-permute-start.3 = (bf16[3,1,128,512]{3,2,1,0:T(8,128)(2,1)S(1)}, bf16[3,1,128,512]{3,2,1,0:T(8,128)(2,1)S(1)}, u32[]{:S(2)}, u32[]{:S(2)}) collective-permute-start(bf16[3,1,128,512]{3,2,1,0:T(8,128)(2,1)S(1)} %pad_maximum_fusion.5), channel_id=1, source_target_pairs={{1,0},{2,1},{3,2},{0,3},{5,4},{6,5},{7,6},{4,7},{9,8},{10,9},{11,1... | collective-permute-start | bytes 1179656 | tf_op jit(solution)/shard_map/ppermute | solution.py:21
  136.6 6.7 %collective-permute-start.4 = (bf16[3,64,512]{2,1,0:T(8,128)(2,1)S(1)}, bf16[3,64,512]{2,1,0:T(8,128)(2,1)S(1)}, u32[]{:S(2)}, u32[]{:S(2)}) collective-permute-start(bf16[3,64,512]{2,1,0:T(8,128)(2,1)S(1)} %bitcast.79), channel_id=1, source_target_pairs={{0,28},{4,0},{8,4},{12,8},{16,12},{20,16},{24,20},{28,24},{1,29},{... | collective-permute-start | bytes 589832 | tf_op jit(solution)/shard_map/ppermute | solution.py:31
  138.4 9.2 %collective-permute-start.5 = (bf16[3,64,512]{2,1,0:T(8,128)(2,1)S(1)}, bf16[3,64,512]{2,1,0:T(8,128)(2,1)S(1)}, u32[]{:S(2)}, u32[]{:S(2)}) collective-permute-start(bf16[3,64,512]{2,1,0:T(8,128)(2,1)S(1)} %bitcast.78), channel_id=1, source_target_pairs={{0,4},{4,8},{8,12},{12,16},{16,20},{20,24},{24,28},{28,0},{1,5},{5... | collective-permute-start | bytes 589832 | tf_op jit(solution)/shard_map/ppermute | solution.py:31
  147.7 4.4 %collective-permute-start.6 = (bf16[64,512]{1,0:T(8,128)(2,1)S(1)}, bf16[64,512]{1,0:T(8,128)(2,1)S(1)}, u32[]{:S(2)}, u32[]{:S(2)}) collective-permute-start(bf16[64,512]{1,0:T(8,128)(2,1)S(1)} %get-tuple-element.14), channel_id=1, source_target_pairs={{0,3},{1,0},{2,1},{3,2},{4,7},{5,4},{6,5},{7,6},{8,11},{9,8},{10,9... | collective-permute-start | bytes 196616 | tf_op jit(solution)/shard_map/ppermute | solution.py:31
  152.1 9.5 %collective-permute-start.8 = (bf16[1,1,64,512]{3,2,1,0:T(8,128)(2,1)S(1)}, bf16[1,1,64,512]{3,2,1,0:T(8,128)(2,1)S(1)}, u32[]{:S(2)}, u32[]{:S(2)}) collective-permute-start(bf16[1,1,64,512]{3,2,1,0:T(8,128)(2,1)S(1)} %bitcast.64), channel_id=1, source_target_pairs={{0,4},{4,8},{8,12},{12,16},{16,20},{20,24},{24,28},{28,0},{1,5},{5... | collective-permute-start | bytes 196616 | tf_op jit(solution)/shard_map/ppermute | solution.py:19
  152.1 9.4 %collective-permute-start.9 = (bf16[1,1,64,512]{3,2,1,0:T(8,128)(2,1)S(1)}, bf16[1,1,64,512]{3,2,1,0:T(8,128)(2,1)S(1)}, u32[]{:S(2)}, u32[]{:S(2)}) collective-permute-start(bf16[1,1,64,512]{3,2,1,0:T(8,128)(2,1)S(1)} %bitcast.65), channel_id=1, source_target_pairs={{4,0},{8,4},{12,8},{16,12},{20,16},{24,20},{28,24},{0,28},{5,1},{9... | collective-permute-start | bytes 196616 | tf_op jit(solution)/shard_map/ppermute | solution.py:21
  161.6 5.8 %collective-permute-start.10 = (bf16[3,1,64,512]{3,2,1,0:T(8,128)(2,1)S(1)}, bf16[3,1,64,512]{3,2,1,0:T(8,128)(2,1)S(1)}, u32[]{:S(2)}, u32[]{:S(2)}) collective-permute-start(bf16[3,1,64,512]{3,2,1,0:T(8,128)(2,1)S(1)} %pad_maximum_fusion.10), channel_id=1, source_target_pairs={{0,1},{1,2},{2,3},{3,0},{4,5},{5,6},{6,7},{7,4},{8,9},{9,10},{10,1... | collective-permute-start | bytes 589832 | tf_op jit(solution)/shard_map/ppermute | solution.py:19
  163.9 5.8 %collective-permute-start.11 = (bf16[3,1,64,512]{3,2,1,0:T(8,128)(2,1)S(1)}, bf16[3,1,64,512]{3,2,1,0:T(8,128)(2,1)S(1)}, u32[]{:S(2)}, u32[]{:S(2)}) collective-permute-start(bf16[3,1,64,512]{3,2,1,0:T(8,128)(2,1)S(1)} %pad_maximum_fusion.10), channel_id=1, source_target_pairs={{1,0},{2,1},{3,2},{0,3},{5,4},{6,5},{7,6},{4,7},{9,8},{10,9},{11,1... | collective-permute-start | bytes 589832 | tf_op jit(solution)/shard_map/ppermute | solution.py:21
  186.6 4.5 %collective-permute-start.12 = (bf16[3,32,512]{2,1,0:T(8,128)(2,1)S(1)}, bf16[3,32,512]{2,1,0:T(8,128)(2,1)S(1)}, u32[]{:S(2)}, u32[]{:S(2)}) collective-permute-start(bf16[3,32,512]{2,1,0:T(8,128)(2,1)S(1)} %bitcast.81), channel_id=1, source_target_pairs={{0,28},{4,0},{8,4},{12,8},{16,12},{20,16},{24,20},{28,24},{1,29},{... | collective-permute-start | bytes 294920 | tf_op jit(solution)/shard_map/ppermute | solution.py:31
  188.1 7.4 %collective-permute-start.13 = (bf16[3,32,512]{2,1,0:T(8,128)(2,1)S(1)}, bf16[3,32,512]{2,1,0:T(8,128)(2,1)S(1)}, u32[]{:S(2)}, u32[]{:S(2)}) collective-permute-start(bf16[3,32,512]{2,1,0:T(8,128)(2,1)S(1)} %bitcast.80), channel_id=1, source_target_pairs={{0,4},{4,8},{8,12},{12,16},{16,20},{20,24},{24,28},{28,0},{1,5},{5... | collective-permute-start | bytes 294920 | tf_op jit(solution)/shard_map/ppermute | solution.py:31
  199.0 5.5 %collective-permute-start.16 = (bf16[1,1,32,512]{3,2,1,0:T(8,128)(2,1)S(1)}, bf16[1,1,32,512]{3,2,1,0:T(8,128)(2,1)S(1)}, u32[]{:S(2)}, u32[]{:S(2)}) collective-permute-start(bf16[1,1,32,512]{3,2,1,0:T(8,128)(2,1)S(1)} %bitcast.71), channel_id=1, source_target_pairs={{0,4},{4,8},{8,12},{12,16},{16,20},{20,24},{24,28},{28,0},{1,5},{5... | collective-permute-start | bytes 98312 | tf_op jit(solution)/shard_map/ppermute | solution.py:19
  199.1 5.5 %collective-permute-start.17 = (bf16[1,1,32,512]{3,2,1,0:T(8,128)(2,1)S(1)}, bf16[1,1,32,512]{3,2,1,0:T(8,128)(2,1)S(1)}, u32[]{:S(2)}, u32[]{:S(2)}) collective-permute-start(bf16[1,1,32,512]{3,2,1,0:T(8,128)(2,1)S(1)} %bitcast.72), channel_id=1, source_target_pairs={{4,0},{8,4},{12,8},{16,12},{20,16},{24,20},{28,24},{0,28},{5,1},{9... | collective-permute-start | bytes 98312 | tf_op jit(solution)/shard_map/ppermute | solution.py:21
  204.5 6.1 %collective-permute-start.18 = (bf16[3,1,32,512]{3,2,1,0:T(8,128)(2,1)S(1)}, bf16[3,1,32,512]{3,2,1,0:T(8,128)(2,1)S(1)}, u32[]{:S(2)}, u32[]{:S(2)}) collective-permute-start(bf16[3,1,32,512]{3,2,1,0:T(8,128)(2,1)S(1)} %pad_maximum_fusion.12), channel_id=1, source_target_pairs={{0,1},{1,2},{2,3},{3,0},{4,5},{5,6},{6,7},{7,4},{8,9},{9,10},{10,1... | collective-permute-start | bytes 294920 | tf_op jit(solution)/shard_map/ppermute | solution.py:19
  207.5 4.0 %collective-permute-start.19 = (bf16[3,1,32,512]{3,2,1,0:T(8,128)(2,1)S(1)}, bf16[3,1,32,512]{3,2,1,0:T(8,128)(2,1)S(1)}, u32[]{:S(2)}, u32[]{:S(2)}) collective-permute-start(bf16[3,1,32,512]{3,2,1,0:T(8,128)(2,1)S(1)} %pad_maximum_fusion.12), channel_id=1, source_target_pairs={{1,0},{2,1},{3,2},{0,3},{5,4},{6,5},{7,6},{4,7},{9,8},{10,9},{11,1... | collective-permute-start | bytes 294920 | tf_op jit(solution)/shard_map/ppermute | solution.py:21
  219.9 6.1 %collective-permute-start.20 = (bf16[1,1,32,512]{3,2,1,0:T(8,128)(2,1)S(1)}, bf16[1,1,32,512]{3,2,1,0:T(8,128)(2,1)S(1)}, u32[]{:S(2)}, u32[]{:S(2)}) collective-permute-start(bf16[1,1,32,512]{3,2,1,0:T(8,128)(2,1)S(1)} %slice_bitcast_fusion.5), channel_id=1, source_target_pairs={{0,4},{4,8},{8,12},{12,16},{16,20},{20,24},{24,28},{28,0},{1,5},{5... | collective-permute-start | bytes 98312 | tf_op jit(solution)/shard_map/ppermute | solution.py:19
  220.0 6.1 %collective-permute-start.21 = (bf16[1,1,32,512]{3,2,1,0:T(8,128)(2,1)S(1)}, bf16[1,1,32,512]{3,2,1,0:T(8,128)(2,1)S(1)}, u32[]{:S(2)}, u32[]{:S(2)}) collective-permute-start(bf16[1,1,32,512]{3,2,1,0:T(8,128)(2,1)S(1)} %slice_bitcast_fusion.5), channel_id=1, source_target_pairs={{4,0},{8,4},{12,8},{16,12},{20,16},{24,20},{28,24},{0,28},{5,1},{9... | collective-permute-start | bytes 98312 | tf_op jit(solution)/shard_map/ppermute | solution.py:21
  227.5 4.0 %collective-permute-start.23 = (bf16[3,1,32,512]{3,2,1,0:T(8,128)(2,1)S(1)}, bf16[3,1,32,512]{3,2,1,0:T(8,128)(2,1)S(1)}, u32[]{:S(2)}, u32[]{:S(2)}) collective-permute-start(bf16[3,1,32,512]{3,2,1,0:T(8,128)(2,1)S(1)} %pad_maximum_fusion.13), channel_id=1, source_target_pairs={{1,0},{2,1},{3,2},{0,3},{5,4},{6,5},{7,6},{4,7},{9,8},{10,9},{11,1... | collective-permute-start | bytes 294920 | tf_op jit(solution)/shard_map/ppermute | solution.py:21
  232.9 6.7 %collective-permute-start.24 = (bf16[1,1,64,512]{3,2,1,0:T(8,128)(2,1)S(1)}, bf16[1,1,64,512]{3,2,1,0:T(8,128)(2,1)S(1)}, u32[]{:S(2)}, u32[]{:S(2)}) collective-permute-start(bf16[1,1,64,512]{3,2,1,0:T(8,128)(2,1)S(1)} %slice_bitcast_fusion.1), channel_id=1, source_target_pairs={{0,4},{4,8},{8,12},{12,16},{16,20},{20,24},{24,28},{28,0},{1,5},{5... | collective-permute-start | bytes 196616 | tf_op jit(solution)/shard_map/ppermute | solution.py:19
  233.0 6.6 %collective-permute-start.25 = (bf16[1,1,64,512]{3,2,1,0:T(8,128)(2,1)S(1)}, bf16[1,1,64,512]{3,2,1,0:T(8,128)(2,1)S(1)}, u32[]{:S(2)}, u32[]{:S(2)}) collective-permute-start(bf16[1,1,64,512]{3,2,1,0:T(8,128)(2,1)S(1)} %slice_bitcast_fusion.1), channel_id=1, source_target_pairs={{4,0},{8,4},{12,8},{16,12},{20,16},{24,20},{28,24},{0,28},{5,1},{9... | collective-permute-start | bytes 196616 | tf_op jit(solution)/shard_map/ppermute | solution.py:21
  239.6 4.6 %collective-permute-start.26 = (bf16[3,1,64,512]{3,2,1,0:T(8,128)(2,1)S(1)}, bf16[3,1,64,512]{3,2,1,0:T(8,128)(2,1)S(1)}, u32[]{:S(2)}, u32[]{:S(2)}) collective-permute-start(bf16[3,1,64,512]{3,2,1,0:T(8,128)(2,1)S(1)} %pad_maximum_fusion.11), channel_id=1, source_target_pairs={{0,1},{1,2},{2,3},{3,0},{4,5},{5,6},{6,7},{7,4},{8,9},{9,10},{10,1... | collective-permute-start | bytes 589832 | tf_op jit(solution)/shard_map/ppermute | solution.py:19
  240.7 5.8 %collective-permute-start.27 = (bf16[3,1,64,512]{3,2,1,0:T(8,128)(2,1)S(1)}, bf16[3,1,64,512]{3,2,1,0:T(8,128)(2,1)S(1)}, u32[]{:S(2)}, u32[]{:S(2)}) collective-permute-start(bf16[3,1,64,512]{3,2,1,0:T(8,128)(2,1)S(1)} %pad_maximum_fusion.11), channel_id=1, source_target_pairs={{1,0},{2,1},{3,2},{0,3},{5,4},{6,5},{7,6},{4,7},{9,8},{10,9},{11,1... | collective-permute-start | bytes 589832 | tf_op jit(solution)/shard_map/ppermute | solution.py:21
  (46 other events, 348.7 us)
where the time goes:
time: 255 us; the launch traced here: 254 us
  local copies, waits for them, and re-layouts  82.2 us (32%)
  matrix products  64.1 us (25%)
  waiting for transfers between devices  47.6 us (19%)
  starting transfers between devices  40.3 us (16%)
  other arithmetic  18.9 us (7%)
    dot_general x6, matrix products, finish(): jnp.dot(hidden, project_out, preferred_element_type=jnp.float32)  30.8 us
    gather x1, local copies, waits for them, and re-layouts, per_device(): jnp.take(source_proj, fine_src, axis=0)  28.8 us
    gather x1, local copies, waits for them, and re-layouts, per_device(): jnp.take(target_proj, fine_dst, axis=0)  24.7 us
    ppermute x10, starting transfers between devices, padded(): lax.ppermute(head, axis, [((i + 1) % count, i) for i in range(count)])  21 us
    dot_general x3, matrix products, node_update(): jnp.dot(incoming.astype(jnp.bfloat16), update_in[features:], preferred_el...  20.3 us
    ppermute x8, waiting for transfers between devices, passed_along(): return lax.ppermute(value, axis, pairs)  19.8 us
    ppermute x10, waiting for transfers between devices, padded(): lax.ppermute(tail, axis, [(i, (i + 1) % count) for i in range(count)])  18.7 us
    ppermute x10, starting transfers between devices, padded(): lax.ppermute(tail, axis, [(i, (i + 1) % count) for i in range(count)])  12.2 us
  transfers between devices with their start and end apart: 28, of which 18 were waited for; matrix products, arithmetic and copies ran while one was open for 19% of the time, Pallas kernels for 0%

commit v1 on v0

--- a/solution.py
+++ b/solution.py
@@ -1,12 +1,122 @@
 import jax
 import jax.numpy as jnp
 from jax import lax
+from jax.experimental import pallas as pl
+from jax.experimental.pallas import tpu as pltpu
 from jax.sharding import PartitionSpec as P
 
 NC1_DEV = 256
 NC2_DEV = 64
 CB1 = 64
 CB2 = 32
+
+
+def ln(pre, gain):
+    mean = jnp.mean(pre, axis=-1, keepdims=True)
+    c = pre - mean
+    var = jnp.mean(c*c, axis=-1, keepdims=True)
+    return c * lax.rsqrt(var + 1e-05) * gain
+
+def silu(x):
+    return x / (1.0 + jnp.exp(-x))
+
+def dotf(a, b):
+    return jnp.dot(a, b, preferred_element_type=jnp.float32)
+
+
+def make_fine(nodes, edges, feats, bnd, own1, ext1, B=256, sub=256):
+    lanes = 128
+    C = feats // lanes
+    steps = edges // (2*B)
+    nsrc = nodes + 9*bnd
+
+    def put(tab, start, val):
+        n = val.shape[0]
+        for c in range(C):
+            tab[pl.ds(start*C + c, n, stride=C), :] = val[:, c*lanes:(c+1)*lanes]
+
+    def kernel(src_ref, dsts_ref, fn_ref, gxm, gxp, gym, gyp, lat_ref, dstv_ref, par_ref, wt_ref,
+               win_ref, wout_ref, gain_ref, uin_ref, uout_ref, ugain_ref,
+               new_ref, own_ref, blk_ref, tab_s, tab_d, g0, g1, acc):
+        i = pl.program_id(0)
+
+        def gather(base, g):
+            for j in range(B):
+                s = src_ref[base + j]
+                d = dsts_ref[base + j]
+                g[C*j:C*(j+1), :] = (tab_s[pl.ds(pl.multiple_of(s*C, C), C), :]
+                                     + tab_d[pl.ds(pl.multiple_of(d*C, C), C), :])
+
+        @pl.when(i == 0)
+        def _():
+            ws = win_ref[:feats, :]
+            put(tab_s, 0, dotf(fn_ref[...], ws))
+            put(tab_d, 0, dotf(fn_ref[...], win_ref[feats:2*feats, :]))
+            a = dotf(gym[...], ws); b = dotf(gyp[...], ws)
+            for t in range(3):
+                put(tab_s, nodes + (3*t)*bnd, a[t*bnd:(t+1)*bnd])
+                put(tab_s, nodes + (3*t+2)*bnd, b[t*bnd:(t+1)*bnd])
+            put(tab_s, nodes + bnd, dotf(gxm[...], ws))
+            put(tab_s, nodes + 7*bnd, dotf(gxp[...], ws))
+            acc[...] = jnp.zeros_like(acc)
+            gather(0, g0)
+
+        def block(h, g):
+            msgs = []
+            for r in range(0, B, sub):
+                pre = dotf(lat_ref[h*B + r:h*B + r + sub, :], win_ref[2*feats:, :])
+                pre = pre + jnp.concatenate(
+                    [g[pl.ds(C*r + c, sub, stride=C), :] for c in range(C)], axis=1)
+                hid = silu(pre).astype(jnp.bfloat16)
+                m = ln(dotf(hid, wout_ref[...]), gain_ref[...].astype(jnp.float32))
+                msgs.append(m.astype(jnp.bfloat16))
+            msg = jnp.concatenate(msgs, axis=0) if len(msgs) > 1 else msgs[0]
+            d = dstv_ref[:, h*B:(h+1)*B]
+            for n0 in range(0, nodes, 256):
+                oh = (lax.broadcasted_iota(jnp.int32, (256, B), 0) + n0 == d).astype(jnp.bfloat16)
+                acc[n0:n0+256, :] += dotf(oh, msg)
+
+        gather((2*i+1)*B, g1)
+        block(0, g0)
+        gather(jnp.minimum(2*i+2, 2*steps-1)*B, g0)
+        block(1, g1)
+
+        @pl.when(i == steps-1)
+        def _():
+            gain = ugain_ref[...].astype(jnp.float32)
+            for n0 in range(0, nodes, 256):
+                st = fn_ref[n0:n0+256, :]
+                pre = dotf(st, uin_ref[:feats, :]) + dotf(acc[n0:n0+256, :].astype(jnp.bfloat16), uin_ref[feats:, :])
+                hid = silu(pre).astype(jnp.bfloat16)
+                new_ref[n0:n0+256, :] = (st.astype(jnp.float32) + ln(dotf(hid, uout_ref[...]), gain)).astype(jnp.bfloat16)
+            for n0 in range(0, ext1, 64):
+                sel = lax.broadcasted_iota(jnp.int32, (64, nodes), 0) + n0 == par_ref[...]
+                sm = jnp.where(sel, wt_ref[...].astype(jnp.float32), 0.0).astype(jnp.bfloat16)
+                out = dotf(sm, new_ref[...])
+                if n0 < own1:
+                    own_ref[n0:n0+64, :] = out
+                else:
+                    blk_ref[n0-own1:n0-own1+64, :] = out.astype(jnp.bfloat16)
+
+    full = lambda *s: pl.BlockSpec(s, lambda i, *_: (0,)*len(s))
+    grid_spec = pltpu.PrefetchScalarGridSpec(
+        num_scalar_prefetch=2, grid=(steps,),
+        in_specs=[full(nodes, feats), full(bnd, feats), full(bnd, feats), full(3*bnd, feats), full(3*bnd, feats),
+                  pl.BlockSpec((2*B, feats), lambda i, *_: (i, 0)),
+                  pl.BlockSpec((1, 2*B), lambda i, *_: (0, i)),
+                  full(1, nodes), full(1, nodes),
+                  full(3*feats, feats), full(feats, feats), full(1, feats),
+                  full(2*feats, feats), full(feats, feats), full(1, feats)],
+        out_specs=[full(nodes, feats), full(own1, feats), full(ext1-own1, feats)],
+        scratch_shapes=[pltpu.VMEM((nsrc*C, lanes), jnp.float32), pltpu.VMEM((nodes*C, lanes), jnp.float32),
+                        pltpu.VMEM((B*C, lanes), jnp.float32), pltpu.VMEM((B*C, lanes), jnp.float32),
+                        pltpu.VMEM((nodes, feats), jnp.float32)])
+    return pl.pallas_call(kernel, grid_spec=grid_spec,
+        out_shape=[jax.ShapeDtypeStruct((nodes, feats), jnp.bfloat16),
+                   jax.ShapeDtypeStruct((own1, feats), jnp.float32),
+                   jax.ShapeDtypeStruct((ext1-own1, feats), jnp.bfloat16)],
+        compiler_params=pltpu.CompilerParams(dimension_semantics=("arbitrary",), vmem_limit_bytes=60*1024*1024),
+        name="fine_stage")
 
 
 def padded(cells, sides, width):
@@ -91,28 +201,30 @@
     return node_update(owned_rows, incoming, update_in, update_out, update_gain)
 
 
+def gathered_sums(own_sums, beyond, rim_count):
+    features = own_sums.shape[1]
+    blocks = beyond.reshape(3, 3, rim_count, features)
+    column = blocks[:, 1].astype(jnp.float32)
+    for step_y in (-1, 1):
+        column = column + passed_along(blocks[:, step_y + 1], "gy", step_y).astype(jnp.float32)
+    inbound = column[1]
+    for step_x in (-1, 1):
+        inbound = inbound + passed_along(
+            column[step_x + 1].astype(jnp.bfloat16), "gx", step_x
+        ).astype(jnp.float32)
+    owned = jnp.concatenate([own_sums[:rim_count] + inbound, own_sums[rim_count:]], axis=0)
+    return owned.astype(jnp.bfloat16)
+
+
 def restrict(states, parents, weights, local_count, rim_count):
-    features = states.shape[1]
     positions = lax.iota(jnp.int32, local_count + 9 * rim_count)
     spread_matrix = jnp.where(
         positions[:, None] == parents[None, :], weights[None, :], jnp.zeros((), jnp.bfloat16)
     )
     spread_sums = jnp.dot(spread_matrix, states, preferred_element_type=jnp.float32)
-    blocks = spread_sums[local_count:].reshape(3, 3, rim_count, features)
-    column = blocks[1]
-    for step_x in (-1, 1):
-        column = column + passed_along(
-            blocks[step_x + 1].astype(jnp.bfloat16), "gx", step_x
-        ).astype(jnp.float32)
-    inbound = column[1]
-    for step_y in (-1, 1):
-        inbound = inbound + passed_along(
-            column[step_y + 1].astype(jnp.bfloat16), "gy", step_y
-        ).astype(jnp.float32)
-    owned = jnp.concatenate(
-        [spread_sums[:rim_count] + inbound, spread_sums[rim_count:local_count]], axis=0
-    )
-    return owned.astype(jnp.bfloat16)
+    return gathered_sums(
+        spread_sums[:local_count], spread_sums[local_count:].astype(jnp.bfloat16), rim_count
+    )
 
 
 def per_device(
@@ -142,30 +254,24 @@
     coarse_update_out,
     coarse_update_gain,
 ):
-    features = fine_nodes.shape[1]
-    edge_rows = jnp.take(fine_nodes, boundary, axis=0)
-    beside_all = padded(edge_rows[None, None], (("gx", 0), ("gy", 1)), 1)
-    source_weights = fine_message_in[:features]
-    own_proj = jnp.dot(fine_nodes, source_weights, preferred_element_type=jnp.float32)
-    target_proj = jnp.dot(
-        fine_nodes, fine_message_in[features : 2 * features], preferred_element_type=jnp.float32
-    )
-    latent_proj = jnp.dot(
-        edge_latent, fine_message_in[2 * features :], preferred_element_type=jnp.float32
-    )
-    around_proj = jnp.dot(
-        beside_all.reshape(-1, features), source_weights, preferred_element_type=jnp.float32
-    )
-    source_proj = jnp.concatenate([own_proj, around_proj], axis=0)
-    preact = (
-        jnp.take(source_proj, fine_src, axis=0)
-        + jnp.take(target_proj, fine_dst, axis=0)
-        + latent_proj
-    )
-    messages = finish(preact, fine_message_out, fine_message_gain).astype(jnp.bfloat16)
-    incoming = summed(fine_dst, messages, fine_nodes.shape[0])
-    fine_new = node_update(fine_nodes, incoming, fine_update_in, fine_update_out, fine_update_gain)
-    level_one = restrict(fine_new, parent_one, weight_one, NC1_DEV, CB1)
+    nodes, features = fine_nodes.shape
+    rim = boundary.shape[0]
+    pick = (boundary[:, None] == lax.iota(jnp.int32, nodes)[None, :]).astype(jnp.bfloat16)
+    edge_rows = dotf(pick, fine_nodes).astype(jnp.bfloat16)
+    from_left = passed_along(edge_rows, "gx", 1)
+    from_right = passed_along(edge_rows, "gx", -1)
+    stack = jnp.concatenate([from_left, edge_rows, from_right], axis=0)
+    from_below = passed_along(stack, "gy", 1)
+    from_above = passed_along(stack, "gy", -1)
+    fine_new, own_sums, beyond = make_fine(
+        nodes, edge_latent.shape[0], features, rim, NC1_DEV, NC1_DEV + 9 * CB1, B=512, sub=512
+    )(
+        fine_src, fine_dst, fine_nodes, from_left, from_right, from_below, from_above,
+        edge_latent, fine_dst[None, :], parent_one[None, :], weight_one[None, :],
+        fine_message_in, fine_message_out, fine_message_gain[None, :],
+        fine_update_in, fine_update_out, fine_update_gain[None, :],
+    )
+    level_one = gathered_sums(own_sums, beyond, CB1)
     level_one_new = coarse_level(
         level_one,
         extend_rows(level_one, CB1),

time: 255 us -> 188 us (0.74)
  local copies, waits for them, and re-layouts: 82.2 us -> 28.7 us
  matrix products: 64.1 us -> 17.6 us
  Pallas kernels: 0 us -> 38 us
  waiting for transfers between devices: 47.6 us -> 43.4 us
  other arithmetic: 18.9 us -> 14.9 us
  starting transfers between devices: 40.3 us -> 43.7 us
    gather x3 -> x0, local copies, waits for them, and re-layouts: 55.7 us -> none  [the longest x1 28.8 us: per_device(): jnp.take(source_proj, fine_src, axis=0)]
    pallas_call x0 -> x1, Pallas kernels: none -> 38 us  [per_device(): make_fine(nodes, edge_latent.shape[0], features, rim, NC1_DEV, NC1_DEV +...]
    dot_general x6 -> x4, matrix products: 30.8 us -> 7.57 us  [finish(): jnp.dot(hidden, project_out, preferred_element_type=jnp.float32)]
    dot_general x3 -> x2, matrix products: 20.3 us -> 4.75 us  [node_update(): jnp.dot(incoming.astype(jnp.bfloat16), update_in[features:], preferred_el...]
    ppermute x8 -> x12, starting transfers between devices: 7.09 us -> 14.4 us  [passed_along(): return lax.ppermute(value, axis, pairs)]
    reduce_sum x6 -> x4, other arithmetic: 7.41 us -> 1.03 us  [normed(): spread = jnp.mean(centred * centred, axis=-1, keepdims=True)]
    ppermute x10 -> x8, waiting for transfers between devices: 18.7 us -> 13 us  [padded(): lax.ppermute(tail, axis, [(i, (i + 1) % count) for i in range(count)])]
    dot_general x3 -> x1, matrix products: 6.98 us -> 1.64 us  [dotf(): return jnp.dot(a, b, preferred_element_type=jnp.float32)]
  transfers between devices with their start and end apart: 28 -> 28, of which waited for: 18 -> 18; matrix products, arithmetic and copies ran while one was open for 19% -> 13% of each run, Pallas kernels for 0% -> 0%
where the time goes in v1:
time: 188 us; the launch traced here: 187 us
  starting transfers between devices  43.7 us (23%)
  waiting for transfers between devices  43.4 us (23%)
  Pallas kernels  38 us (20%)
  local copies, waits for them, and re-layouts  28.7 us (15%)
  matrix products  17.6 us (9%)
  other arithmetic  14.9 us (8%)
    pallas_call x1, Pallas kernels, per_device(): make_fine(nodes, edge_latent.shape[0], features, rim, NC1_DEV, NC1_DEV +...  38 us
    ppermute x12, waiting for transfers between devices, passed_along(): return lax.ppermute(value, axis, pairs)  24.1 us
    ppermute x8, starting transfers between devices, padded(): lax.ppermute(head, axis, [((i + 1) % count, i) for i in range(count)])  17.4 us
    ppermute x12, starting transfers between devices, passed_along(): return lax.ppermute(value, axis, pairs)  14.4 us
    ppermute x8, waiting for transfers between devices, padded(): lax.ppermute(tail, axis, [(i, (i + 1) % count) for i in range(count)])  13 us
    ppermute x8, starting transfers between devices, padded(): lax.ppermute(tail, axis, [(i, (i + 1) % count) for i in range(count)])  11.9 us
    dot_general x4, matrix products, finish(): jnp.dot(hidden, project_out, preferred_element_type=jnp.float32)  7.57 us
    gather x2, local copies, waits for them, and re-layouts, coarse_level(): jnp.take(source_proj, sources, axis=0)  7.22 us
  transfers between devices with their start and end apart: 28, of which 18 were waited for; matrix products, arithmetic and copies ran while one was open for 13% of the time, Pallas kernels for 0%

profile of v1, /device:TPU:1, one launch (start us, length us, event | category | flops | bytes accessed | tf_op | source)
XLA Modules:
  0.0 187.1 jit_solution(5073867562767048222)
XLA Ops:
  3.8 3.1 %collective-permute-start.1 = (bf16[128,512]{1,0:T(8,128)(2,1)S(1)}, bf16[128,512]{1,0:T(8,128)(2,1)S(1)}, u32[]{:S(2)}, u32[]{:S(2)}) collective-permute-start(bf16[128,512]{1,0:T(8,128)(2,1)S(1)} %convolution_convert_fusion), channel_id=1, source_target_pairs={{0,28},{4,0},{8,4},{12,8},{16,12},{20,16},{24,20},{28,24},{1,29},{... | collective-permute-start | bytes 393224 | tf_op jit(solution)/shard_map/ppermute | solution.py:141
  17.1 2.2 %collective-permute-start.2 = (bf16[384,512]{1,0:T(8,128)(2,1)S(1)}, bf16[384,512]{1,0:T(8,128)(2,1)S(1)}, u32[]{:S(2)}, u32[]{:S(2)}) collective-permute-start(bf16[384,512]{1,0:T(8,128)(2,1)S(1)} %pad_maximum_fusion.3), channel_id=1, source_target_pairs={{0,1},{1,2},{2,3},{3,0},{4,5},{5,6},{6,7},{7,4},{8,9},{9,10},{10,1... | collective-permute-start | bytes 1179656 | tf_op jit(solution)/shard_map/ppermute | solution.py:141
  21.9 5.6 %collective-permute-done.2.gym = bf16[384,512]{1,0:T(8,128)(2,1)S(1)} collective-permute-done((bf16[384,512]{1,0:T(8,128)(2,1)S(1)}, bf16[384,512]{1,0:T(8,128)(2,1)S(1)}, u32[]{:S(2)}, u32[]{:S(2)}) %collective-permute-start.2) | collective-permute-done | bytes 393248 | tf_op jit(solution)/shard_map/ppermute | solution.py:141
  29.6 38.0 %fine_stage.1 = (bf16[1024,512]{1,0:T(8,128)(2,1)}, f32[256,512]{1,0:T(8,128)}, bf16[576,512]{1,0:T(8,128)(2,1)}) custom-call(s32[6144]{0:T(1024)} %src_ref.1, s32[6144]{0:T(1024)} %dsts_ref.1, bf16[1024,512]{1,0:T(8,128)(2,1)} %fn_ref.1, bf16[128,512]{1,0:T(8,128)(2,1)} %copy-done.9, bf16[128,512]{1,0:T(8,128)(2,1)} %copy-done.10, ...), custom_call_target="tpu_custom_call" | custom-call | tf_op jit(solution)/shard_map/fine_stage/pallas_call | solution.py:266
  71.0 4.1 %collective-permute-done.4 = bf16[3,64,512]{2,1,0:T(8,128)(2,1)S(1)} collective-permute-done((bf16[3,64,512]{2,1,0:T(8,128)(2,1)S(1)}, bf16[3,64,512]{2,1,0:T(8,128)(2,1)S(1)}, u32[]{:S(2)}, u32[]{:S(2)}) %collective-permute-start.4) | collective-permute-done | bytes 196640 | tf_op jit(solution)/shard_map/ppermute | solution.py:141
  79.4 4.5 %collective-permute-done.7 = bf16[64,512]{1,0:T(8,128)(2,1)S(1)} collective-permute-done((bf16[64,512]{1,0:T(8,128)(2,1)S(1)}, bf16[64,512]{1,0:T(8,128)(2,1)S(1)}, u32[]{:S(2)}, u32[]{:S(2)}) %collective-permute-start.7) | collective-permute-done | bytes 65568 | tf_op jit(solution)/shard_map/ppermute | solution.py:141
  84.9 4.2 %collective-permute-start.9 = (bf16[1,1,64,512]{3,2,1,0:T(8,128)(2,1)S(1)}, bf16[1,1,64,512]{3,2,1,0:T(8,128)(2,1)S(1)}, u32[]{:S(2)}, u32[]{:S(2)}) collective-permute-start(bf16[1,1,64,512]{3,2,1,0:T(8,128)(2,1)S(1)} %bitcast.83), channel_id=1, source_target_pairs={{4,0},{8,4},{12,8},{16,12},{20,16},{24,20},{28,24},{0,28},{5,1},{9... | collective-permute-start | bytes 196616 | tf_op jit(solution)/shard_map/ppermute | solution.py:131
  89.4 4.9 %gather_fusion.1 = f32[1536,512]{1,0:T(8,128)} fusion(f32[256,512]{1,0:T(8,128)S(1)} %fusion.18, s32[2048]{0:T(1024)S(1)} %pad_clamp_fusion), kind=kCustom, calls=%fused_computation.1 | custom fusion | bytes 6297600 | tf_op jit(solution)/shard_map/jit(_take)/gather | solution.py:198
  94.3 4.4 %collective-permute-start.10 = (bf16[3,1,64,512]{3,2,1,0:T(8,128)(2,1)S(1)}, bf16[3,1,64,512]{3,2,1,0:T(8,128)(2,1)S(1)}, u32[]{:S(2)}, u32[]{:S(2)}) collective-permute-start(bf16[3,1,64,512]{3,2,1,0:T(8,128)(2,1)S(1)} %pad_maximum_fusion.8), channel_id=1, source_target_pairs={{0,1},{1,2},{2,3},{3,0},{4,5},{5,6},{6,7},{7,4},{8,9},{9,10},{10,1... | collective-permute-start | bytes 589832 | tf_op jit(solution)/shard_map/ppermute | solution.py:129
  99.8 2.7 %collective-permute-done.10 = bf16[3,1,64,512]{3,2,1,0:T(8,128)(2,1)S(1)} collective-permute-done((bf16[3,1,64,512]{3,2,1,0:T(8,128)(2,1)S(1)}, bf16[3,1,64,512]{3,2,1,0:T(8,128)(2,1)S(1)}, u32[]{:S(2)}, u32[]{:S(2)}) %collective-permute-start.10) | collective-permute-done | bytes 196640 | tf_op jit(solution)/shard_map/ppermute | solution.py:129
  104.9 5.0 %gather_fusion = f32[1536,512]{1,0:T(8,128)} fusion(f32[832,512]{1,0:T(8,128)S(1)} %fusion.6, s32[2048]{0:T(1024)S(1)} %pad_clamp_fusion.1), kind=kCustom, calls=%fused_computation | custom fusion | bytes 6297600 | tf_op jit(solution)/shard_map/jit(_take)/gather | solution.py:198
  109.9 4.8 %fusion.76 = (f32[1536]{0:T(1024)S(1)}, f32[1536,512]{0,1:T(8,128)S(1)}) fusion(bf16[512,512]{1,0:T(8,128)(2,1)S(1)} %copy-done, f32[1536,512]{1,0:T(8,128)} %gather_fusion.1, f32[1536,512]{1,0:T(8,128)} %gather_fusion, pred[1536]{0:T(1024)(128)(4,1)S(1)} %copy-done.26, pred[1536]{0:T(1024)(128)(4,1)S(1)} %copy-done.27), kind=kOutput, calls=%fused_computation.149 | convolution fusion | flops 812382720 | bytes 9970688 | tf_op jit(solution)/shard_map/dot_general | solution.py:153
  116.8 3.1 %multiply_convert_fusion.10 = bf16[256,512]{1,0:T(8,128)(2,1)S(1)} fusion(f32[256,512]{1,0:T(8,128)S(1)} %copy-done.11, f32[1536,512]{0,1:T(8,128)} %copy-done.1, f32[512]{0:T(512)S(1)} %copy-done.28, f32[1536]{0:T(1024)S(1)} %add_rsqrt_fusion, f32[1536]{0:T(1024)S(1)} %broadcast_multiply_fusion, s32[1536]{0:T(1024)S(1)} %copy-done.18, ...), kind=kOutput, calls=%fused_computation.37 | convolution fusion | flops 541327360 | bytes 4476928 | tf_op jit(solution)/shard_map/dot_general | solution.py:164
  122.9 2.8 %collective-permute-done.12 = bf16[3,32,512]{2,1,0:T(8,128)(2,1)S(1)} collective-permute-done((bf16[3,32,512]{2,1,0:T(8,128)(2,1)S(1)}, bf16[3,32,512]{2,1,0:T(8,128)(2,1)S(1)}, u32[]{:S(2)}, u32[]{:S(2)}) %collective-permute-start.12) | collective-permute-done | bytes 98336 | tf_op jit(solution)/shard_map/ppermute | solution.py:141
  128.6 4.1 %collective-permute-done.15 = bf16[32,512]{1,0:T(8,128)(2,1)S(1)} collective-permute-done((bf16[32,512]{1,0:T(8,128)(2,1)S(1)}, bf16[32,512]{1,0:T(8,128)(2,1)S(1)}, u32[]{:S(2)}, u32[]{:S(2)}) %collective-permute-start.15) | collective-permute-done | bytes 32800 | tf_op jit(solution)/shard_map/ppermute | solution.py:141
  132.8 4.1 %collective-permute-start.17 = (bf16[1,1,32,512]{3,2,1,0:T(8,128)(2,1)S(1)}, bf16[1,1,32,512]{3,2,1,0:T(8,128)(2,1)S(1)}, u32[]{:S(2)}, u32[]{:S(2)}) collective-permute-start(bf16[1,1,32,512]{3,2,1,0:T(8,128)(2,1)S(1)} %bitcast.91), channel_id=1, source_target_pairs={{4,0},{8,4},{12,8},{16,12},{20,16},{24,20},{28,24},{0,28},{5,1},{9... | collective-permute-start | bytes 98312 | tf_op jit(solution)/shard_map/ppermute | solution.py:131
  138.3 4.8 %collective-permute-start.18 = (bf16[3,1,32,512]{3,2,1,0:T(8,128)(2,1)S(1)}, bf16[3,1,32,512]{3,2,1,0:T(8,128)(2,1)S(1)}, u32[]{:S(2)}, u32[]{:S(2)}) collective-permute-start(bf16[3,1,32,512]{3,2,1,0:T(8,128)(2,1)S(1)} %pad_maximum_fusion.10), channel_id=1, source_target_pairs={{0,1},{1,2},{2,3},{3,0},{4,5},{5,6},{6,7},{7,4},{8,9},{9,10},{10,1... | collective-permute-start | bytes 294920 | tf_op jit(solution)/shard_map/ppermute | solution.py:129
  144.0 2.2 %gather_fusion.3 = f32[384,512]{1,0:T(8,128)} fusion(f32[64,512]{1,0:T(8,128)S(1)} %fusion.16, s32[1024]{0:T(1024)S(1)} %pad_clamp_fusion.3), kind=kCustom, calls=%fused_computation.3 | custom fusion | bytes 1574400 | tf_op jit(solution)/shard_map/jit(_take)/gather | solution.py:198
  147.6 2.3 %gather_fusion.2 = f32[384,512]{1,0:T(8,128)} fusion(f32[352,512]{1,0:T(8,128)S(1)} %fusion.20, s32[1024]{0:T(1024)S(1)} %pad_clamp_fusion.4), kind=kCustom, calls=%fused_computation.2 | custom fusion | bytes 1574400 | tf_op jit(solution)/shard_map/jit(_take)/gather | solution.py:198
  155.5 4.5 %collective-permute-start.21 = (bf16[1,1,32,512]{3,2,1,0:T(8,128)(2,1)S(1)}, bf16[1,1,32,512]{3,2,1,0:T(8,128)(2,1)S(1)}, u32[]{:S(2)}, u32[]{:S(2)}) collective-permute-start(bf16[1,1,32,512]{3,2,1,0:T(8,128)(2,1)S(1)} %slice_bitcast_fusion.11), channel_id=1, source_target_pairs={{4,0},{8,4},{12,8},{16,12},{20,16},{24,20},{28,24},{0,28},{5,1},{9... | collective-permute-start | bytes 98312 | tf_op jit(solution)/shard_map/ppermute | solution.py:131
  164.7 2.4 %collective-permute-done.23 = bf16[3,1,32,512]{3,2,1,0:T(8,128)(2,1)S(1)} collective-permute-done((bf16[3,1,32,512]{3,2,1,0:T(8,128)(2,1)S(1)}, bf16[3,1,32,512]{3,2,1,0:T(8,128)(2,1)S(1)}, u32[]{:S(2)}, u32[]{:S(2)}) %collective-permute-start.23) | collective-permute-done | bytes 98336 | tf_op jit(solution)/shard_map/ppermute | solution.py:131
  168.5 4.6 %collective-permute-start.25 = (bf16[1,1,64,512]{3,2,1,0:T(8,128)(2,1)S(1)}, bf16[1,1,64,512]{3,2,1,0:T(8,128)(2,1)S(1)}, u32[]{:S(2)}, u32[]{:S(2)}) collective-permute-start(bf16[1,1,64,512]{3,2,1,0:T(8,128)(2,1)S(1)} %slice_bitcast_fusion.7), channel_id=1, source_target_pairs={{4,0},{8,4},{12,8},{16,12},{20,16},{24,20},{28,24},{0,28},{5,1},{9... | collective-permute-start | bytes 196616 | tf_op jit(solution)/shard_map/ppermute | solution.py:131
  176.3 4.0 %collective-permute-done.26 = bf16[3,1,64,512]{3,2,1,0:T(8,128)(2,1)S(1)} collective-permute-done((bf16[3,1,64,512]{3,2,1,0:T(8,128)(2,1)S(1)}, bf16[3,1,64,512]{3,2,1,0:T(8,128)(2,1)S(1)}, u32[]{:S(2)}, u32[]{:S(2)}) %collective-permute-start.26) | collective-permute-done | bytes 196640 | tf_op jit(solution)/shard_map/ppermute | solution.py:129
  181.7 4.0 %gather_fusion.5 = bf16[1024,512]{1,0:T(8,128)(2,1)S(1)} fusion(bf16[832,512]{1,0:T(8,128)(2,1)S(1)} %pad_maximum_fusion, s32[1024]{0:T(1024)S(1)} %fusion.60), kind=kCustom, calls=%fused_computation.5 | custom fusion | bytes 2101248 | tf_op jit(solution)/shard_map/jit(_take)/gather | solution.py:180
  (177 shorter events, 60.0 us)
Async XLA Ops:
  1.7 15.4 %collective-permute-start = (bf16[128,512]{1,0:T(8,128)(2,1)S(1)}, bf16[128,512]{1,0:T(8,128)(2,1)S(1)}, u32[]{:S(2)}, u32[]{:S(2)}) collective-permute-start(bf16[128,512]{1,0:T(8,128)(2,1)S(1)} %convolution_convert_fusion), channel_id=1, source_target_pairs={{0,4},{4,8},{8,12},{12,16},{16,20},{20,24},{24,28},{28,0},{1,5},{5... | collective-permute-start | bytes 393224 | tf_op jit(solution)/shard_map/ppermute | solution.py:141
  3.8 13.3 %collective-permute-start.1 = (bf16[128,512]{1,0:T(8,128)(2,1)S(1)}, bf16[128,512]{1,0:T(8,128)(2,1)S(1)}, u32[]{:S(2)}, u32[]{:S(2)}) collective-permute-start(bf16[128,512]{1,0:T(8,128)(2,1)S(1)} %convolution_convert_fusion), channel_id=1, source_target_pairs={{0,28},{4,0},{8,4},{12,8},{16,12},{20,16},{24,20},{28,24},{1,29},{... | collective-permute-start | bytes 393224 | tf_op jit(solution)/shard_map/ppermute | solution.py:141
  17.1 10.4 %collective-permute-start.2 = (bf16[384,512]{1,0:T(8,128)(2,1)S(1)}, bf16[384,512]{1,0:T(8,128)(2,1)S(1)}, u32[]{:S(2)}, u32[]{:S(2)}) collective-permute-start(bf16[384,512]{1,0:T(8,128)(2,1)S(1)} %pad_maximum_fusion.3), channel_id=1, source_target_pairs={{0,1},{1,2},{2,3},{3,0},{4,5},{5,6},{6,7},{7,4},{8,9},{9,10},{10,1... | collective-permute-start | bytes 1179656 | tf_op jit(solution)/shard_map/ppermute | solution.py:141
  19.3 9.5 %collective-permute-start.3 = (bf16[384,512]{1,0:T(8,128)(2,1)S(1)}, bf16[384,512]{1,0:T(8,128)(2,1)S(1)}, u32[]{:S(2)}, u32[]{:S(2)}) collective-permute-start(bf16[384,512]{1,0:T(8,128)(2,1)S(1)} %pad_maximum_fusion.3), channel_id=1, source_target_pairs={{0,3},{1,0},{2,1},{3,2},{4,7},{5,4},{6,5},{7,6},{8,11},{9,8},{10,9... | collective-permute-start | bytes 1179656 | tf_op jit(solution)/shard_map/ppermute | solution.py:141
  68.7 6.5 %collective-permute-start.4 = (bf16[3,64,512]{2,1,0:T(8,128)(2,1)S(1)}, bf16[3,64,512]{2,1,0:T(8,128)(2,1)S(1)}, u32[]{:S(2)}, u32[]{:S(2)}) collective-permute-start(bf16[3,64,512]{2,1,0:T(8,128)(2,1)S(1)} %get-tuple-element.15), channel_id=1, source_target_pairs={{0,3},{1,0},{2,1},{3,2},{4,7},{5,4},{6,5},{7,6},{8,11},{9,8},{10,9... | collective-permute-start | bytes 589832 | tf_op jit(solution)/shard_map/ppermute | solution.py:141
  68.7 6.5 %collective-permute-start.5 = (bf16[3,64,512]{2,1,0:T(8,128)(2,1)S(1)}, bf16[3,64,512]{2,1,0:T(8,128)(2,1)S(1)}, u32[]{:S(2)}, u32[]{:S(2)}) collective-permute-start(bf16[3,64,512]{2,1,0:T(8,128)(2,1)S(1)} %get-tuple-element.16), channel_id=1, source_target_pairs={{0,1},{1,2},{2,3},{3,0},{4,5},{5,6},{6,7},{7,4},{8,9},{9,10},{10,1... | collective-permute-start | bytes 589832 | tf_op jit(solution)/shard_map/ppermute | solution.py:141
  78.1 5.8 %collective-permute-start.7 = (bf16[64,512]{1,0:T(8,128)(2,1)S(1)}, bf16[64,512]{1,0:T(8,128)(2,1)S(1)}, u32[]{:S(2)}, u32[]{:S(2)}) collective-permute-start(bf16[64,512]{1,0:T(8,128)(2,1)S(1)} %get-tuple-element.20), channel_id=1, source_target_pairs={{0,4},{4,8},{8,12},{12,16},{16,20},{20,24},{24,28},{28,0},{1,5},{5... | collective-permute-start | bytes 196616 | tf_op jit(solution)/shard_map/ppermute | solution.py:141
  84.8 9.5 %collective-permute-start.8 = (bf16[1,1,64,512]{3,2,1,0:T(8,128)(2,1)S(1)}, bf16[1,1,64,512]{3,2,1,0:T(8,128)(2,1)S(1)}, u32[]{:S(2)}, u32[]{:S(2)}) collective-permute-start(bf16[1,1,64,512]{3,2,1,0:T(8,128)(2,1)S(1)} %bitcast.82), channel_id=1, source_target_pairs={{0,4},{4,8},{8,12},{12,16},{16,20},{20,24},{24,28},{28,0},{1,5},{5... | collective-permute-start | bytes 196616 | tf_op jit(solution)/shard_map/ppermute | solution.py:129
  84.9 9.4 %collective-permute-start.9 = (bf16[1,1,64,512]{3,2,1,0:T(8,128)(2,1)S(1)}, bf16[1,1,64,512]{3,2,1,0:T(8,128)(2,1)S(1)}, u32[]{:S(2)}, u32[]{:S(2)}) collective-permute-start(bf16[1,1,64,512]{3,2,1,0:T(8,128)(2,1)S(1)} %bitcast.83), channel_id=1, source_target_pairs={{4,0},{8,4},{12,8},{16,12},{20,16},{24,20},{28,24},{0,28},{5,1},{9... | collective-permute-start | bytes 196616 | tf_op jit(solution)/shard_map/ppermute | solution.py:131
  94.3 8.2 %collective-permute-start.10 = (bf16[3,1,64,512]{3,2,1,0:T(8,128)(2,1)S(1)}, bf16[3,1,64,512]{3,2,1,0:T(8,128)(2,1)S(1)}, u32[]{:S(2)}, u32[]{:S(2)}) collective-permute-start(bf16[3,1,64,512]{3,2,1,0:T(8,128)(2,1)S(1)} %pad_maximum_fusion.8), channel_id=1, source_target_pairs={{0,1},{1,2},{2,3},{3,0},{4,5},{5,6},{6,7},{7,4},{8,9},{9,10},{10,1... | collective-permute-start | bytes 589832 | tf_op jit(solution)/shard_map/ppermute | solution.py:129
  98.7 5.5 %collective-permute-start.11 = (bf16[3,1,64,512]{3,2,1,0:T(8,128)(2,1)S(1)}, bf16[3,1,64,512]{3,2,1,0:T(8,128)(2,1)S(1)}, u32[]{:S(2)}, u32[]{:S(2)}) collective-permute-start(bf16[3,1,64,512]{3,2,1,0:T(8,128)(2,1)S(1)} %pad_maximum_fusion.8), channel_id=1, source_target_pairs={{1,0},{2,1},{3,2},{0,3},{5,4},{6,5},{7,6},{4,7},{9,8},{10,9},{11,1... | collective-permute-start | bytes 589832 | tf_op jit(solution)/shard_map/ppermute | solution.py:131
  121.1 4.6 %collective-permute-start.12 = (bf16[3,32,512]{2,1,0:T(8,128)(2,1)S(1)}, bf16[3,32,512]{2,1,0:T(8,128)(2,1)S(1)}, u32[]{:S(2)}, u32[]{:S(2)}) collective-permute-start(bf16[3,32,512]{2,1,0:T(8,128)(2,1)S(1)} %get-tuple-element.17), channel_id=1, source_target_pairs={{0,3},{1,0},{2,1},{3,2},{4,7},{5,4},{6,5},{7,6},{8,11},{9,8},{10,9... | collective-permute-start | bytes 294920 | tf_op jit(solution)/shard_map/ppermute | solution.py:141
  121.2 4.6 %collective-permute-start.13 = (bf16[3,32,512]{2,1,0:T(8,128)(2,1)S(1)}, bf16[3,32,512]{2,1,0:T(8,128)(2,1)S(1)}, u32[]{:S(2)}, u32[]{:S(2)}) collective-permute-start(bf16[3,32,512]{2,1,0:T(8,128)(2,1)S(1)} %get-tuple-element.18), channel_id=1, source_target_pairs={{0,1},{1,2},{2,3},{3,0},{4,5},{5,6},{6,7},{7,4},{8,9},{9,10},{10,1... | collective-permute-start | bytes 294920 | tf_op jit(solution)/shard_map/ppermute | solution.py:141
  127.3 5.5 %collective-permute-start.15 = (bf16[32,512]{1,0:T(8,128)(2,1)S(1)}, bf16[32,512]{1,0:T(8,128)(2,1)S(1)}, u32[]{:S(2)}, u32[]{:S(2)}) collective-permute-start(bf16[32,512]{1,0:T(8,128)(2,1)S(1)} %get-tuple-element.22), channel_id=1, source_target_pairs={{0,4},{4,8},{8,12},{12,16},{16,20},{20,24},{24,28},{28,0},{1,5},{5... | collective-permute-start | bytes 98312 | tf_op jit(solution)/shard_map/ppermute | solution.py:141
  132.8 5.5 %collective-permute-start.16 = (bf16[1,1,32,512]{3,2,1,0:T(8,128)(2,1)S(1)}, bf16[1,1,32,512]{3,2,1,0:T(8,128)(2,1)S(1)}, u32[]{:S(2)}, u32[]{:S(2)}) collective-permute-start(bf16[1,1,32,512]{3,2,1,0:T(8,128)(2,1)S(1)} %bitcast.90), channel_id=1, source_target_pairs={{0,4},{4,8},{8,12},{12,16},{16,20},{20,24},{24,28},{28,0},{1,5},{5... | collective-permute-start | bytes 98312 | tf_op jit(solution)/shard_map/ppermute | solution.py:129
  132.8 5.5 %collective-permute-start.17 = (bf16[1,1,32,512]{3,2,1,0:T(8,128)(2,1)S(1)}, bf16[1,1,32,512]{3,2,1,0:T(8,128)(2,1)S(1)}, u32[]{:S(2)}, u32[]{:S(2)}) collective-permute-start(bf16[1,1,32,512]{3,2,1,0:T(8,128)(2,1)S(1)} %bitcast.91), channel_id=1, source_target_pairs={{4,0},{8,4},{12,8},{16,12},{20,16},{24,20},{28,24},{0,28},{5,1},{9... | collective-permute-start | bytes 98312 | tf_op jit(solution)/shard_map/ppermute | solution.py:131
  138.3 8.0 %collective-permute-start.18 = (bf16[3,1,32,512]{3,2,1,0:T(8,128)(2,1)S(1)}, bf16[3,1,32,512]{3,2,1,0:T(8,128)(2,1)S(1)}, u32[]{:S(2)}, u32[]{:S(2)}) collective-permute-start(bf16[3,1,32,512]{3,2,1,0:T(8,128)(2,1)S(1)} %pad_maximum_fusion.10), channel_id=1, source_target_pairs={{0,1},{1,2},{2,3},{3,0},{4,5},{5,6},{6,7},{7,4},{8,9},{9,10},{10,1... | collective-permute-start | bytes 294920 | tf_op jit(solution)/shard_map/ppermute | solution.py:129
  155.5 6.4 %collective-permute-start.20 = (bf16[1,1,32,512]{3,2,1,0:T(8,128)(2,1)S(1)}, bf16[1,1,32,512]{3,2,1,0:T(8,128)(2,1)S(1)}, u32[]{:S(2)}, u32[]{:S(2)}) collective-permute-start(bf16[1,1,32,512]{3,2,1,0:T(8,128)(2,1)S(1)} %slice_bitcast_fusion.11), channel_id=1, source_target_pairs={{0,4},{4,8},{8,12},{12,16},{16,20},{20,24},{24,28},{28,0},{1,5},{5... | collective-permute-start | bytes 98312 | tf_op jit(solution)/shard_map/ppermute | solution.py:129
  155.5 6.4 %collective-permute-start.21 = (bf16[1,1,32,512]{3,2,1,0:T(8,128)(2,1)S(1)}, bf16[1,1,32,512]{3,2,1,0:T(8,128)(2,1)S(1)}, u32[]{:S(2)}, u32[]{:S(2)}) collective-permute-start(bf16[1,1,32,512]{3,2,1,0:T(8,128)(2,1)S(1)} %slice_bitcast_fusion.11), channel_id=1, source_target_pairs={{4,0},{8,4},{12,8},{16,12},{20,16},{24,20},{28,24},{0,28},{5,1},{9... | collective-permute-start | bytes 98312 | tf_op jit(solution)/shard_map/ppermute | solution.py:131
  163.0 4.0 %collective-permute-start.23 = (bf16[3,1,32,512]{3,2,1,0:T(8,128)(2,1)S(1)}, bf16[3,1,32,512]{3,2,1,0:T(8,128)(2,1)S(1)}, u32[]{:S(2)}, u32[]{:S(2)}) collective-permute-start(bf16[3,1,32,512]{3,2,1,0:T(8,128)(2,1)S(1)} %pad_maximum_fusion.11), channel_id=1, source_target_pairs={{1,0},{2,1},{3,2},{0,3},{5,4},{6,5},{7,6},{4,7},{9,8},{10,9},{11,1... | collective-permute-start | bytes 294920 | tf_op jit(solution)/shard_map/ppermute | solution.py:131
  168.5 6.4 %collective-permute-start.24 = (bf16[1,1,64,512]{3,2,1,0:T(8,128)(2,1)S(1)}, bf16[1,1,64,512]{3,2,1,0:T(8,128)(2,1)S(1)}, u32[]{:S(2)}, u32[]{:S(2)}) collective-permute-start(bf16[1,1,64,512]{3,2,1,0:T(8,128)(2,1)S(1)} %slice_bitcast_fusion.7), channel_id=1, source_target_pairs={{0,4},{4,8},{8,12},{12,16},{16,20},{20,24},{24,28},{28,0},{1,5},{5... | collective-permute-start | bytes 196616 | tf_op jit(solution)/shard_map/ppermute | solution.py:129
  168.5 6.3 %collective-permute-start.25 = (bf16[1,1,64,512]{3,2,1,0:T(8,128)(2,1)S(1)}, bf16[1,1,64,512]{3,2,1,0:T(8,128)(2,1)S(1)}, u32[]{:S(2)}, u32[]{:S(2)}) collective-permute-start(bf16[1,1,64,512]{3,2,1,0:T(8,128)(2,1)S(1)} %slice_bitcast_fusion.7), channel_id=1, source_target_pairs={{4,0},{8,4},{12,8},{16,12},{20,16},{24,20},{28,24},{0,28},{5,1},{9... | collective-permute-start | bytes 196616 | tf_op jit(solution)/shard_map/ppermute | solution.py:131
  174.9 5.4 %collective-permute-start.26 = (bf16[3,1,64,512]{3,2,1,0:T(8,128)(2,1)S(1)}, bf16[3,1,64,512]{3,2,1,0:T(8,128)(2,1)S(1)}, u32[]{:S(2)}, u32[]{:S(2)}) collective-permute-start(bf16[3,1,64,512]{3,2,1,0:T(8,128)(2,1)S(1)} %pad_maximum_fusion.9), channel_id=1, source_target_pairs={{0,1},{1,2},{2,3},{3,0},{4,5},{5,6},{6,7},{7,4},{8,9},{9,10},{10,1... | collective-permute-start | bytes 589832 | tf_op jit(solution)/shard_map/ppermute | solution.py:129
  176.2 5.3 %collective-permute-start.27 = (bf16[3,1,64,512]{3,2,1,0:T(8,128)(2,1)S(1)}, bf16[3,1,64,512]{3,2,1,0:T(8,128)(2,1)S(1)}, u32[]{:S(2)}, u32[]{:S(2)}) collective-permute-start(bf16[3,1,64,512]{3,2,1,0:T(8,128)(2,1)S(1)} %pad_maximum_fusion.9), channel_id=1, source_target_pairs={{1,0},{2,1},{3,2},{0,3},{5,4},{6,5},{7,6},{4,7},{9,8},{10,9},{11,1... | collective-permute-start | bytes 589832 | tf_op jit(solution)/shard_map/ppermute | solution.py:131
  (36 other events, 397.7 us)

commit v2 on v0

v2 whole, which is shorter than its diff:
```python
import jax
import jax.numpy as jnp
from jax import lax
from jax.experimental import pallas as pl
from jax.experimental.pallas import tpu as pltpu
from jax.sharding import PartitionSpec as P

NC1_DEV = 256
NC2_DEV = 64
CB1 = 64
CB2 = 32
LANES = 128
VMEM_BYTES = 40 * 1024 * 1024
PART_DTYPE = jnp.float32

VSPEC = pl.BlockSpec(memory_space=pltpu.VMEM)
SSPEC = pl.BlockSpec(memory_space=pltpu.SMEM)


def in_hbm(value):
    return pltpu.with_memory_space_constraint(value, pltpu.HBM)


def whole(*shape):
    return pl.BlockSpec(shape, lambda i, *_: (0,) * len(shape))


def params(grid=False):
    return pltpu.CompilerParams(
        dimension_semantics=("arbitrary",) if grid else None, vmem_limit_bytes=VMEM_BYTES
    )


def passed_along(value, axis, steps):
    count = lax.axis_size(axis)
    pairs = [(source, (source + steps) % count) for source in range(count)]
    return lax.ppermute(value, axis, pairs)


def dotf(a, b):
    return jnp.dot(a, b, preferred_element_type=jnp.float32)


def normed(preact, gain):
    centred = preact - jnp.mean(preact, axis=-1, keepdims=True)
    spread = jnp.mean(centred * centred, axis=-1, keepdims=True)
    return centred * lax.rsqrt(spread + 1e-05) * gain


def silu(value):
    half = 0.5 * value
    return half + half * jnp.tanh(half)


def put_rows(table, start, rows):
    count, features = rows.shape
    C = features // LANES
    for c in range(C):
        table[pl.ds(start * C + c, count, stride=C), :] = rows[:, c * LANES : (c + 1) * LANES]


def get_rows(lines, start, count, C):
    return jnp.concatenate(
        [lines[pl.ds(start * C + c, count, stride=C), :] for c in range(C)], axis=1
    )


def line(table, row, C):
    return table[pl.ds(pl.multiple_of(row * C, C), C), :]


def spread(lines, reads, C):
    for j, read in enumerate(reads):
        lines[C * j : C * (j + 1), :] = read()


def onehot_sum(targets, messages, first, count):
    hits = lax.broadcasted_iota(jnp.int32, (count, messages.shape[0]), 0) + first == targets
    return dotf(hits.astype(jnp.bfloat16), messages)


def update_rows(states, incoming, update_in, update_out, gain):
    features = states.shape[1]
    preact = dotf(states, update_in[:features, :]) + dotf(
        incoming.astype(jnp.bfloat16), update_in[features:, :]
    )
    hidden = silu(preact).astype(jnp.bfloat16)
    return (states.astype(jnp.float32) + normed(dotf(hidden, update_out[...]), gain)).astype(
        jnp.bfloat16
    )


def restrict_into(states, parents, weights, local_count, rim_count, own, up, mid, down):
    total = local_count + 9 * rim_count
    hits = lax.broadcasted_iota(jnp.int32, (total, states.shape[0]), 0) == parents
    spread = jnp.where(hits, weights.astype(jnp.float32), 0.0).astype(jnp.bfloat16)
    sums = dotf(spread, states)
    own[...] = sums[:local_count]
    for dx in range(3):
        for dy, ref in ((0, down), (1, mid), (2, up)):
            k = 3 * dx + dy
            rows = sums[local_count + k * rim_count : local_count + (k + 1) * rim_count]
            if k == 4:
                rows = sums[:rim_count]
            ref[dx * rim_count : (dx + 1) * rim_count, :] = rows.astype(ref.dtype)


def restrict_shapes(local_count, rim_count, features):
    return [
        jax.ShapeDtypeStruct((local_count, features), jnp.float32),
        jax.ShapeDtypeStruct((3 * rim_count, features), jnp.bfloat16),
        jax.ShapeDtypeStruct((3 * rim_count, features), jnp.float32),
        jax.ShapeDtypeStruct((3 * rim_count, features), jnp.bfloat16),
    ]


def edge_start(dst, nodes_in, latent, message_in, block, begin, blocks, part=None):
    nodes, features = nodes_in.shape
    edges = latent.shape[0]
    C = features // LANES
    opening = part is None

    def kernel(dst_ref, node_ref, latent_ref, in_ref, *rest):
        part_ref = rest[0 if opening else 1]
        table, lines0, lines1 = rest[-3:]
        step = pl.program_id(0)

        def gather(at, lines):
            base = (begin + jnp.minimum(at, blocks - 1)) * block
            spread(lines, [lambda j=j: line(table, dst_ref[base + j], C) for j in range(block)], C)

        def project(half, lines):
            rows = slice(half * block, (half + 1) * block)
            part_ref[rows, :] = (
                dotf(latent_ref[rows, :], in_ref[2 * features :, :]) + get_rows(lines, 0, block, C)
            ).astype(part_ref.dtype)

        @pl.when(step == 0)
        def _():
            put_rows(table, 0, dotf(node_ref[...], in_ref[features : 2 * features, :]))
            if opening:
                put_rows(rest[1], 0, dotf(node_ref[...], in_ref[:features, :]))
            gather(0, lines0)

        gather(2 * step + 1, lines1)
        project(0, lines0)
        gather(2 * step + 2, lines0)
        project(1, lines1)

    start = begin // 2
    tile = pl.BlockSpec((2 * block, features), lambda i, *_: (i + start, 0))
    part_shape = jax.ShapeDtypeStruct((edges, features), PART_DTYPE)
    return pl.pallas_call(
        kernel,
        grid_spec=pltpu.PrefetchScalarGridSpec(
            num_scalar_prefetch=1,
            grid=(blocks // 2,),
            in_specs=[whole(nodes, features), tile, whole(3 * features, features)] + ([] if opening else [pl.BlockSpec(memory_space=pl.ANY)]),
            out_specs=[tile, VSPEC] if opening else tile,
            scratch_shapes=[
                pltpu.VMEM((nodes * C, LANES), jnp.float32),
                pltpu.VMEM((block * C, LANES), jnp.float32),
                pltpu.VMEM((block * C, LANES), jnp.float32),
            ],
        ),
        out_shape=[part_shape, jax.ShapeDtypeStruct((nodes * C, LANES), jnp.float32)]
        if opening
        else part_shape,
        input_output_aliases={} if opening else {4: 0},
        compiler_params=params(True),
        cost_estimate=pl.CostEstimate(
            flops=2 * blocks * block * features * features, transcendentals=0,
            bytes_accessed=6 * blocks * block * features,
        ),
        name="edge_start",
    )(in_hbm(dst), in_hbm(nodes_in), in_hbm(latent), in_hbm(message_in), *(() if opening else (in_hbm(part),)))


def fine_stage(src, dst, nodes_in, own_lines, left, right, below, above, part, parents, weights,
               message_in, message_out, message_gain, update_in, update_out, update_gain, block):
    nodes, features = nodes_in.shape
    rim = left.shape[0]
    edges = part.shape[0]
    steps = edges // (2 * block)
    C = features // LANES

    def kernel(src_ref, node_ref, own_ref, left_ref, right_ref, below_ref, above_ref, part_ref,
               dst_ref, parent_ref, weight_ref, in_ref, out_ref, gain_ref, uin_ref, uout_ref,
               ugain_ref, new_ref, sums_ref, up_ref, mid_ref, down_ref, table, lines0, lines1, acc, sent):
        step = pl.program_id(0)

        def gather(base, lines):
            spread(lines, [lambda j=j: line(table, src_ref[base + j], C) for j in range(block)], C)

        @pl.when(step == 0)
        def _():
            table[: nodes * C, :] = own_ref[...]
            first = in_ref[:features, :]
            low, high = dotf(below_ref[...], first), dotf(above_ref[...], first)
            for t in range(3):
                put_rows(table, nodes + 3 * t * rim, low[t * rim : (t + 1) * rim])
                put_rows(table, nodes + (3 * t + 2) * rim, high[t * rim : (t + 1) * rim])
            put_rows(table, nodes + rim, dotf(left_ref[...], first))
            put_rows(table, nodes + 7 * rim, dotf(right_ref[...], first))
            acc[...] = jnp.zeros_like(acc)
            gather(0, lines0)

        def block_sum(half, lines):
            preact = part_ref[half * block : (half + 1) * block, :].astype(jnp.float32) + get_rows(lines, 0, block, C)
            hidden = silu(preact).astype(jnp.bfloat16)
            messages = normed(dotf(hidden, out_ref[...]), gain_ref[...].astype(jnp.float32))
            sent[half * block : (half + 1) * block, :] = messages.astype(jnp.bfloat16)

        gather((2 * step + 1) * block, lines1)
        block_sum(0, lines0)
        gather(jnp.minimum(2 * step + 2, 2 * steps - 1) * block, lines0)
        block_sum(1, lines1)
        for n in range(0, nodes, 256):
            acc[n : n + 256, :] += onehot_sum(dst_ref[...], sent[...], n, 256)

        @pl.when(step == steps - 1)
        def _():
            gain = ugain_ref[...].astype(jnp.float32)
            new_ref[...] = update_rows(node_ref[...], acc[...], uin_ref, uout_ref, gain)
            restrict_into(new_ref[...], parent_ref[...], weight_ref[...], NC1_DEV, CB1,
                          sums_ref, up_ref, mid_ref, down_ref)

    return pl.pallas_call(
        kernel,
        grid_spec=pltpu.PrefetchScalarGridSpec(
            num_scalar_prefetch=1,
            grid=(steps,),
            in_specs=[
                VSPEC, VSPEC, VSPEC, VSPEC, VSPEC, VSPEC,
                pl.BlockSpec((2 * block, features), lambda i, *_: (i, 0)),
                pl.BlockSpec((1, 2 * block), lambda i, *_: (0, i)),
                VSPEC, VSPEC, VSPEC, VSPEC, VSPEC, VSPEC, VSPEC, VSPEC,
            ],
            out_specs=[VSPEC] * 5,
            scratch_shapes=[
                pltpu.VMEM(((nodes + 9 * rim) * C, LANES), jnp.float32),
                pltpu.VMEM((block * C, LANES), jnp.float32),
                pltpu.VMEM((block * C, LANES), jnp.float32),
                pltpu.VMEM((nodes, features), jnp.float32),
                pltpu.VMEM((2 * block, features), jnp.bfloat16),
            ],
        ),
        out_shape=[jax.ShapeDtypeStruct((nodes, features), jnp.bfloat16)]
        + restrict_shapes(NC1_DEV, CB1, features),
        compiler_params=params(True),
        name="fine_stage",
    )(src, nodes_in, own_lines, left, right, below, above, in_hbm(part), dst[None, :], parents, weights,
      message_in, message_out, message_gain, update_in, update_out, update_gain)


def column_sums(mid, from_below, from_above):
    rim, features = mid.shape[0] // 3, mid.shape[1]

    def kernel(mid_ref, below_ref, above_ref, right_ref, left_ref, far_right_ref, far_left_ref):
        total = (
            mid_ref[...] + below_ref[...].astype(jnp.float32) + above_ref[...].astype(jnp.float32)
        ).astype(jnp.bfloat16)
        right_ref[...] = total[rim:]
        left_ref[...] = total[: 2 * rim]
        far_right_ref[...] = total[2 * rim :]
        far_left_ref[...] = total[:rim]

    return pl.pallas_call(
        kernel,
        in_specs=[VSPEC] * 3,
        out_specs=[VSPEC] * 4,
        out_shape=[jax.ShapeDtypeStruct((n * rim, features), jnp.bfloat16) for n in (2, 2, 1, 1)],
        compiler_params=params(),
        name="column_sums",
    )(mid, from_below, from_above)


def rim_sums(right, left, in_left, in_right, in_far_left, in_far_right):
    rim, features = right.shape[0] // 2, right.shape[1]

    def kernel(right_ref, left_ref, a1, b1, a2, b2, out_ref):
        def add(*parts):
            total = parts[0].astype(jnp.float32)
            for part in parts[1:]:
                total = total + part.astype(jnp.float32)
            return total.astype(jnp.bfloat16)

        out_ref[:rim, :] = add(a1[:rim, :], a2[...], left_ref[:rim, :])
        out_ref[rim : 2 * rim, :] = add(right_ref[:rim, :], a1[rim:, :], b1[:rim, :])
        out_ref[2 * rim :, :] = add(b1[rim:, :], b2[...], right_ref[rim:, :])

    return pl.pallas_call(
        kernel,
        in_specs=[VSPEC] * 6,
        out_specs=VSPEC,
        out_shape=jax.ShapeDtypeStruct((3 * rim, features), jnp.bfloat16),
        compiler_params=params(),
        name="rim_sums",
    )(right, left, in_left, in_right, in_far_left, in_far_right)


def shared_rims(up, mid, down):
    from_below = passed_along(up, "gy", 1)
    from_above = passed_along(down, "gy", -1)
    right, left, far_right, far_left = column_sums(mid, from_below, from_above)
    in_left = passed_along(right, "gx", 1)
    in_right = passed_along(left, "gx", -1)
    in_far_left = passed_along(far_right, "gx", 2)
    in_far_right = passed_along(far_left, "gx", -2)
    rims = rim_sums(right, left, in_left, in_right, in_far_left, in_far_right)
    return rims, passed_along(rims, "gy", 1), passed_along(rims, "gy", -1)


def put_extended(table, local_count, rim_count, line_rows, below_rows, above_rows):
    for t in range(3):
        span = slice(t * rim_count, (t + 1) * rim_count)
        put_rows(table, local_count + 3 * t * rim_count, below_rows[span])
        if t != 1:
            put_rows(table, local_count + (3 * t + 1) * rim_count, line_rows[span])
        put_rows(table, local_count + (3 * t + 2) * rim_count, above_rows[span])


def level_pass(sums, rims, below, above, src, dst, parents, weights, message_in, message_out,
               message_gain, update_in, update_out, update_gain, chunk, block, below_level):
    count, features = sums.shape
    rim = rims.shape[0] // 3
    edges = src.shape[0]
    C = features // LANES

    def kernel(sums_ref, rims_ref, below_ref, above_ref, src_ref, dst_ref, dstv_ref, parent_ref,
               weight_ref, in_ref, out_ref, gain_ref, uin_ref, uout_ref, ugain_ref, *rest):
        outs, (level, table, targets, lines) = rest[:-4], rest[-4:]
        level[:rim, :] = rims_ref[rim : 2 * rim, :]
        level[rim:, :] = sums_ref[rim:, :].astype(jnp.bfloat16)
        first = in_ref[:features, :]
        put_rows(table, 0, dotf(level[...], first))
        put_rows(targets, 0, dotf(level[...], in_ref[features:, :]))
        put_extended(table, count, rim, dotf(rims_ref[...], first), dotf(below_ref[...], first),
                     dotf(above_ref[...], first))

        @pl.loop(0, edges // chunk)
        def _(t):
            for j in range(chunk):
                e = t * chunk + j
                lines[pl.ds(pl.multiple_of(e * C, C), C), :] = line(
                    table, src_ref[e], C
                ) + line(targets, dst_ref[e], C)

        incoming = jnp.zeros((count, features), jnp.float32)
        for start in range(0, edges, block):
            hidden = silu(get_rows(lines, start, block, C)).astype(jnp.bfloat16)
            messages = normed(dotf(hidden, out_ref[...]), gain_ref[...].astype(jnp.float32))
            incoming = incoming + onehot_sum(
                dstv_ref[:, start : start + block], messages.astype(jnp.bfloat16), 0, count
            )
        new = update_rows(level[...], incoming, uin_ref, uout_ref,
                          ugain_ref[...].astype(jnp.float32))
        outs[0][...] = new
        if below_level:
            restrict_into(new, parent_ref[...], weight_ref[...], *below_level, *outs[1:])
        else:
            outs[1][...] = new[:rim]

    shapes = [jax.ShapeDtypeStruct((count, features), jnp.bfloat16)]
    if below_level:
        shapes += restrict_shapes(*below_level, features)
    else:
        shapes += [jax.ShapeDtypeStruct((rim, features), jnp.bfloat16)]
    return pl.pallas_call(
        kernel,
        in_specs=[VSPEC] * 4 + [SSPEC] * 2 + [VSPEC] * 9,
        out_specs=[VSPEC] * len(shapes),
        out_shape=shapes,
        scratch_shapes=[
            pltpu.VMEM((count, features), jnp.bfloat16),
            pltpu.VMEM(((count + 9 * rim) * C, LANES), jnp.float32),
            pltpu.VMEM((count * C, LANES), jnp.float32),
            pltpu.VMEM((edges * C, LANES), jnp.float32),
        ],
        compiler_params=params(),
        name="level_pass",
    )(sums, rims, below, above, src, dst, dst[None, :], parents, weights, message_in, message_out,
      message_gain, update_in, update_out, update_gain)


def lifted(coarse, rims, below, above, parents, states, chunk, rim_out):
    count, features = states.shape
    local_count = coarse.shape[0]
    rim = rims.shape[0] // 3
    C = features // LANES

    def kernel(coarse_ref, rims_ref, below_ref, above_ref, parent_ref, state_ref, *rest):
        outs, (table, lines) = rest[:-2], rest[-2:]
        put_rows(table, 0, coarse_ref[...].astype(jnp.float32))
        put_extended(table, local_count, rim, rims_ref[...].astype(jnp.float32),
                     below_ref[...].astype(jnp.float32), above_ref[...].astype(jnp.float32))

        @pl.loop(0, count // chunk)
        def _(t):
            for j in range(chunk):
                e = t * chunk + j
                lines[pl.ds(pl.multiple_of(e * C, C), C), :] = line(table, parent_ref[e], C)

        result = (state_ref[...].astype(jnp.float32) + get_rows(lines, 0, count, C)).astype(
            jnp.bfloat16
        )
        outs[0][...] = result
        if rim_out:
            outs[1][...] = result[:rim_out]

    shapes = [jax.ShapeDtypeStruct((count, features), jnp.bfloat16)]
    if rim_out:
        shapes.append(jax.ShapeDtypeStruct((rim_out, features), jnp.bfloat16))
    return pl.pallas_call(
        kernel,
        in_specs=[VSPEC] * 4 + [SSPEC, VSPEC],
        out_specs=[VSPEC] * len(shapes),
        out_shape=shapes,
        scratch_shapes=[
            pltpu.VMEM(((local_count + 9 * rim) * C, LANES), jnp.float32),
            pltpu.VMEM((count * C, LANES), jnp.float32),
        ],
        compiler_params=params(),
        name="lifted",
    )(coarse, rims, below, above, parents, states)


def halo(rows):
    left = passed_along(rows, "gx", 1)
    right = passed_along(rows, "gx", -1)
    stack = jnp.concatenate([left, rows, right], axis=0)
    return left, right, stack, passed_along(stack, "gy", 1), passed_along(stack, "gy", -1)


def per_device(
    fine_nodes,
    edge_latent,
    boundary,
    fine_src,
    fine_dst,
    parent_one,
    weight_one,
    coarse_src_one,
    coarse_dst_one,
    parent_two,
    weight_two,
    coarse_src_two,
    coarse_dst_two,
    fine_message_in,
    fine_message_out,
    fine_message_gain,
    fine_update_in,
    fine_update_out,
    fine_update_gain,
    coarse_message_in,
    coarse_message_out,
    coarse_message_gain,
    coarse_update_in,
    coarse_update_out,
    coarse_update_gain,
):
    nodes, features = fine_nodes.shape
    pick = (boundary[:, None] == lax.iota(jnp.int32, nodes)[None, :]).astype(jnp.bfloat16)
    edge_rows = dotf(pick, fine_nodes).astype(jnp.bfloat16)
    half = edge_latent.shape[0] // 1024
    left = passed_along(edge_rows, "gx", 1)
    right = passed_along(edge_rows, "gx", -1)
    part, own_lines = edge_start(fine_dst, fine_nodes, edge_latent, fine_message_in, 512, 0, half)
    left, right, part = lax.optimization_barrier((left, right, part))
    stack = jnp.concatenate([left, edge_rows, right], axis=0)
    below = passed_along(stack, "gy", 1)
    above = passed_along(stack, "gy", -1)
    part = edge_start(
        fine_dst, fine_nodes, edge_latent, fine_message_in, 512, half, half, part
    )
    fine_new, sums, up, mid, down = fine_stage(
        fine_src, fine_dst, fine_nodes, own_lines, left, right, below, above, part,
        parent_one[None, :], weight_one[None, :], fine_message_in, fine_message_out,
        fine_message_gain[None, :], fine_update_in, fine_update_out, fine_update_gain[None, :], 512,
    )
    coarse = (
        coarse_message_in, coarse_message_out, coarse_message_gain[None, :],
        coarse_update_in, coarse_update_out, coarse_update_gain[None, :],
    )
    rims, below, above = shared_rims(up, mid, down)
    level_one_new, sums, up, mid, down = level_pass(
        sums, rims, below, above, coarse_src_one, coarse_dst_one, parent_two[None, :],
        weight_two[None, :], *coarse, 128, 512, (NC2_DEV, CB2),
    )
    rims, below, above = shared_rims(up, mid, down)
    level_two_new, rim_two = level_pass(
        sums, rims, below, above, coarse_src_two, coarse_dst_two, parent_two[None, :],
        weight_two[None, :], *coarse, 128, coarse_src_two.shape[0], None,
    )
    _, _, stack, below, above = halo(rim_two)
    level_one_final, rim_one = lifted(
        level_two_new, stack, below, above, parent_two, level_one_new, 128, CB1
    )
    _, _, stack, below, above = halo(rim_one)
    return lifted(level_one_final, stack, below, above, parent_one, fine_new, 128, 0)[0]


def solution(mesh):
    rows, flat, copied = P(("gx", "gy"), None), P(("gx", "gy")), P()
    in_specs = (rows, rows) + (flat,) * 11 + (copied,) * 12
    return jax.shard_map(
        per_device, mesh=mesh, in_specs=in_specs, out_specs=rows, check_vma=False
    )
```

time: 255 us -> 142 us (0.56)
  local copies, waits for them, and re-layouts: 82.2 us -> 0.2 us
  Pallas kernels: 0 us -> 62.7 us
  matrix products: 64.1 us -> 1.63 us
  other arithmetic: 18.9 us -> 0.03 us
  waiting for transfers between devices: 47.6 us -> 33.4 us
  starting transfers between devices: 40.3 us -> 42.9 us
    gather x10 -> x0, local copies, waits for them, and re-layouts: 75.8 us -> none  [the longest x1 28.8 us: per_device(): jnp.take(source_proj, fine_src, axis=0)]
    pallas_call x0 -> x11, Pallas kernels: none -> 62.7 us  [the longest x1 25.7 us: fine_stage(): pl.pallas_call(kernel, grid_spec=pltpu.PrefetchScalarGridSpec(num_scalar_...]
    dot_general x21 -> x1, matrix products: 64.1 us -> 1.63 us  [dotf(): return jnp.dot(a, b, preferred_element_type=jnp.float32)]
    ppermute x8 -> x28, starting transfers between devices: 7.09 us -> 42.9 us  [passed_along(): return lax.ppermute(value, axis, pairs)]
    ppermute x20 -> x0, starting transfers between devices: 33.2 us -> none  [the longest x10 21 us: padded(): lax.ppermute(head, axis, [((i + 1) % count, i) for i in range(count)])]
    ppermute x20 -> x0, waiting for transfers between devices: 27.8 us -> none  [the longest x10 18.7 us: padded(): lax.ppermute(tail, axis, [(i, (i + 1) % count) for i in range(count)])]
    ppermute x8 -> x28, waiting for transfers between devices: 19.8 us -> 33.4 us  [passed_along(): return lax.ppermute(value, axis, pairs)]
    reduce_sum x6 -> x0, other arithmetic: 7.41 us -> none  [normed(): spread = jnp.mean(centred * centred, axis=-1, keepdims=True)]
  transfers between devices with their start and end apart: 28 -> 28, of which waited for: 18 -> 13; matrix products, arithmetic and copies ran while one was open for 19% -> 0% of each run, Pallas kernels for 0% -> 16%
where the time goes in v2:
time: 142 us; the launch traced here: 141 us
  Pallas kernels  62.7 us (44%)
  starting transfers between devices  42.9 us (30%)
  waiting for transfers between devices  33.4 us (24%)
  matrix products  1.63 us (1%)
    ppermute x28, starting transfers between devices, passed_along(): return lax.ppermute(value, axis, pairs)  42.9 us
    ppermute x28, waiting for transfers between devices, passed_along(): return lax.ppermute(value, axis, pairs)  33.4 us
    pallas_call x1, Pallas kernels, fine_stage(): pl.pallas_call(kernel, grid_spec=pltpu.PrefetchScalarGridSpec(num_scalar_...  25.7 us
    pallas_call x2, Pallas kernels, edge_start(): pl.pallas_call(kernel, grid_spec=pltpu.PrefetchScalarGridSpec(num_scalar_...  21.9 us
    pallas_call x2, Pallas kernels, level_pass(): pl.pallas_call(kernel, in_specs=[VSPEC] * 4 + [SSPEC] * 2 + [VSPEC] * 9,...  11 us
    pallas_call x2, Pallas kernels, lifted(): pl.pallas_call(kernel, in_specs=[VSPEC] * 4 + [SSPEC, VSPEC], out_specs=[...  3.9 us
  transfers between devices with their start and end apart: 28, of which 13 were waited for; matrix products, arithmetic and copies ran while one was open for 0% of the time, Pallas kernels for 16%

profile of v2, /device:TPU:1, one launch (start us, length us, event | category | flops | bytes accessed | tf_op | source)
XLA Modules:
  0.0 141.4 jit_solution(6024799915581052891)
XLA Ops:
  1.6 5.1 %collective-permute-start.1 = (bf16[128,512]{1,0:T(8,128)(2,1)S(1)}, bf16[128,512]{1,0:T(8,128)(2,1)S(1)}, u32[]{:S(2)}, u32[]{:S(2)}) collective-permute-start(bf16[128,512]{1,0:T(8,128)(2,1)S(1)} %convolution_convert_fusion), channel_id=1, source_target_pairs={{0,28},{4,0},{8,4},{12,8},{16,12},{20,16},{24,20},{28,24},{1,29},{... | collective-permute-start | bytes 393224 | tf_op jit(solution)/shard_map/ppermute | solution.py:37
  6.8 11.1 %edge_start.2 = (f32[6144,512]{1,0:T(8,128)}, f32[4096,128]{1,0:T(8,128)S(1)}) custom-call(s32[6144]{0:T(1024)} %dst_ref.5, bf16[1024,512]{1,0:T(8,128)(2,1)} %node_ref.5, bf16[6144,512]{1,0:T(8,128)(2,1)} %latent_ref.3, bf16[1536,512]{1,0:T(8,128)(2,1)} %in_ref.7), custom_call_target="tpu_custom_call" | custom-call | flops 1610612736 | bytes 9437184 | tf_op jit(solution)/shard_map/edge_start/pallas_call | solution.py:153
  20.4 10.9 %edge_start.3.part_ref = f32[6144,512]{1,0:T(8,128)} custom-call(s32[6144]{0:T(1024)} %dst_ref.5, bf16[1024,512]{1,0:T(8,128)(2,1)} %node_ref.5, bf16[6144,512]{1,0:T(8,128)(2,1)} %latent_ref.3, bf16[1536,512]{1,0:T(8,128)(2,1)} %in_ref.7, f32[6144,512]{1,0:T(8,128)} %get-tuple-element.36.rest_0_), custom_call_target="tpu_custom_call", output_to_operand_aliasing={{}: (4, {})} | custom-call | flops 1610612736 | bytes 9437184 | tf_op jit(solution)/shard_map/edge_start/pallas_call | solution.py:153
  31.5 25.7 %fine_stage.1 = (bf16[1024,512]{1,0:T(8,128)(2,1)S(1)}, f32[256,512]{1,0:T(8,128)S(1)}, bf16[192,512]{1,0:T(8,128)(2,1)S(1)}, f32[192,512]{1,0:T(8,128)S(1)}, bf16[192,512]{1,0:T(8,128)(2,1)S(1)}) custom-call(s32[6144]{0:T(1024)S(1)} %copy-done.11, bf16[1024,512]{1,0:T(8,128)(2,1)S(1)} %copy-done, f32[4096,128]{1,0:T(8,128)S(1)} %get-tuple-element.32.own_ref, ...), custom_call_target="tpu_custom_call" | custom-call | tf_op jit(solution)/shard_map/fine_stage/pallas_call | solution.py:228
  57.8 3.5 %collective-permute-done.4.below_ref = bf16[192,512]{1,0:T(8,128)(2,1)S(1)} collective-permute-done((bf16[192,512]{1,0:T(8,128)(2,1)S(1)}, bf16[192,512]{1,0:T(8,128)(2,1)S(1)}, u32[]{:S(2)}, u32[]{:S(2)}) %collective-permute-start.4) | collective-permute-done | bytes 196640 | tf_op jit(solution)/shard_map/ppermute | solution.py:37
  61.2 1.9 %collective-permute-done.5.above_ref = bf16[192,512]{1,0:T(8,128)(2,1)S(1)} collective-permute-done((bf16[192,512]{1,0:T(8,128)(2,1)S(1)}, bf16[192,512]{1,0:T(8,128)(2,1)S(1)}, u32[]{:S(2)}, u32[]{:S(2)}) %collective-permute-start.5) | collective-permute-done | bytes 196640 | tf_op jit(solution)/shard_map/ppermute | solution.py:37
  63.3 4.3 %collective-permute-start.7 = (bf16[128,512]{1,0:T(8,128)(2,1)S(1)}, bf16[128,512]{1,0:T(8,128)(2,1)S(1)}, u32[]{:S(2)}, u32[]{:S(2)}) collective-permute-start(bf16[128,512]{1,0:T(8,128)(2,1)S(1)} %get-tuple-element.42.left_ref), channel_id=1, source_target_pairs={{0,28},{4,0},{8,4},{12,8},{16,12},{20,16},{24,20},{28,24},{1,29},{... | collective-permute-start | bytes 393224 | tf_op jit(solution)/shard_map/ppermute | solution.py:37
  67.6 3.3 %collective-permute-start.9 = (bf16[64,512]{1,0:T(8,128)(2,1)S(1)}, bf16[64,512]{1,0:T(8,128)(2,1)S(1)}, u32[]{:S(2)}, u32[]{:S(2)}) collective-permute-start(bf16[64,512]{1,0:T(8,128)(2,1)S(1)} %get-tuple-element.44), channel_id=1, source_target_pairs={{0,24},{4,28},{8,0},{12,4},{16,8},{20,12},{24,16},{28,20},{1,25},{... | collective-permute-start | bytes 196616 | tf_op jit(solution)/shard_map/ppermute | solution.py:37
  70.9 2.2 %collective-permute-done.8.a2 = bf16[64,512]{1,0:T(8,128)(2,1)S(1)} collective-permute-done((bf16[64,512]{1,0:T(8,128)(2,1)S(1)}, bf16[64,512]{1,0:T(8,128)(2,1)S(1)}, u32[]{:S(2)}, u32[]{:S(2)}) %collective-permute-start.8) | collective-permute-done | bytes 65568 | tf_op jit(solution)/shard_map/ppermute | solution.py:37
  76.1 5.0 %collective-permute-done.11.above_ref = bf16[192,512]{1,0:T(8,128)(2,1)S(1)} collective-permute-done((bf16[192,512]{1,0:T(8,128)(2,1)S(1)}, bf16[192,512]{1,0:T(8,128)(2,1)S(1)}, u32[]{:S(2)}, u32[]{:S(2)}) %collective-permute-start.11) | collective-permute-done | bytes 196640 | tf_op jit(solution)/shard_map/ppermute | solution.py:37
  81.1 7.8 %level_pass.2 = (bf16[256,512]{1,0:T(8,128)(2,1)S(1)}, f32[64,512]{1,0:T(8,128)S(1)}, bf16[96,512]{1,0:T(8,128)(2,1)S(1)}, f32[96,512]{1,0:T(8,128)S(1)}, bf16[96,512]{1,0:T(8,128)(2,1)S(1)}) custom-call(f32[256,512]{1,0:T(8,128)S(1)} %get-tuple-element.37.sums_ref, bf16[192,512]{1,0:T(8,128)(2,1)S(1)} %rim_sums.2.rims_ref, ...), custom_call_target="tpu_custom_call" | custom-call | tf_op jit(solution)/shard_map/level_pass/pallas_call | solution.py:369
  92.1 2.4 %collective-permute-done.13.above_ref = bf16[96,512]{1,0:T(8,128)(2,1)S(1)} collective-permute-done((bf16[96,512]{1,0:T(8,128)(2,1)S(1)}, bf16[96,512]{1,0:T(8,128)(2,1)S(1)}, u32[]{:S(2)}, u32[]{:S(2)}) %collective-permute-start.13) | collective-permute-done | bytes 98336 | tf_op jit(solution)/shard_map/ppermute | solution.py:37
  94.6 4.1 %collective-permute-start.15 = (bf16[64,512]{1,0:T(8,128)(2,1)S(1)}, bf16[64,512]{1,0:T(8,128)(2,1)S(1)}, u32[]{:S(2)}, u32[]{:S(2)}) collective-permute-start(bf16[64,512]{1,0:T(8,128)(2,1)S(1)} %get-tuple-element.50.left_ref), channel_id=1, source_target_pairs={{0,28},{4,0},{8,4},{12,8},{16,12},{20,16},{24,20},{28,24},{1,29},{... | collective-permute-start | bytes 196616 | tf_op jit(solution)/shard_map/ppermute | solution.py:37
  98.7 3.3 %collective-permute-start.17 = (bf16[32,512]{1,0:T(8,128)(2,1)S(1)}, bf16[32,512]{1,0:T(8,128)(2,1)S(1)}, u32[]{:S(2)}, u32[]{:S(2)}) collective-permute-start(bf16[32,512]{1,0:T(8,128)(2,1)S(1)} %get-tuple-element.52), channel_id=1, source_target_pairs={{0,24},{4,28},{8,0},{12,4},{16,8},{20,12},{24,16},{28,20},{1,25},{... | collective-permute-start | bytes 98312 | tf_op jit(solution)/shard_map/ppermute | solution.py:37
  102.0 1.9 %collective-permute-done.16.a2 = bf16[32,512]{1,0:T(8,128)(2,1)S(1)} collective-permute-done((bf16[32,512]{1,0:T(8,128)(2,1)S(1)}, bf16[32,512]{1,0:T(8,128)(2,1)S(1)}, u32[]{:S(2)}, u32[]{:S(2)}) %collective-permute-start.16) | collective-permute-done | bytes 32800 | tf_op jit(solution)/shard_map/ppermute | solution.py:37
  105.7 3.3 %collective-permute-done.19.above_ref = bf16[96,512]{1,0:T(8,128)(2,1)S(1)} collective-permute-done((bf16[96,512]{1,0:T(8,128)(2,1)S(1)}, bf16[96,512]{1,0:T(8,128)(2,1)S(1)}, u32[]{:S(2)}, u32[]{:S(2)}) %collective-permute-start.19) | collective-permute-done | bytes 98336 | tf_op jit(solution)/shard_map/ppermute | solution.py:37
  109.0 3.2 %level_pass.3 = (bf16[64,512]{1,0:T(8,128)(2,1)S(1)}, bf16[32,512]{1,0:T(8,128)(2,1)S(1)}) custom-call(f32[64,512]{1,0:T(8,128)S(1)} %get-tuple-element.45.sums_ref, bf16[96,512]{1,0:T(8,128)(2,1)S(1)} %rim_sums.3.rims_ref, bf16[96,512]{1,0:T(8,128)(2,1)S(1)} %collective-permute-done.18.below_ref, bf16[96,512]{1,0:T(8,128)(2,1)S(1)} %collective-permute-done.19.above_ref, ...), custom_call_target="tpu_custom_call" | custom-call | tf_op jit(solution)/shard_map/level_pass/pallas_call | solution.py:369
  112.3 4.1 %collective-permute-start.21 = (bf16[32,512]{1,0:T(8,128)(2,1)S(1)}, bf16[32,512]{1,0:T(8,128)(2,1)S(1)}, u32[]{:S(2)}, u32[]{:S(2)}) collective-permute-start(bf16[32,512]{1,0:T(8,128)(2,1)S(1)} %get-tuple-element.54), channel_id=1, source_target_pairs={{0,28},{4,0},{8,4},{12,8},{16,12},{20,16},{24,20},{28,24},{1,29},{... | collective-permute-start | bytes 98312 | tf_op jit(solution)/shard_map/ppermute | solution.py:37
  117.8 1.9 %collective-permute-start.23 = (bf16[96,512]{1,0:T(8,128)(2,1)S(1)}, bf16[96,512]{1,0:T(8,128)(2,1)S(1)}, u32[]{:S(2)}, u32[]{:S(2)}) collective-permute-start(bf16[96,512]{1,0:T(8,128)(2,1)S(1)} %constant_dynamic-update-slice_fusion.rims_ref), channel_id=1, source_target_pairs={{0,3},{1,0},{2,1},{3,2},{4,7},{5,4},{6,5},{7,6},{8,11},{9,8},{10,9... | collective-permute-start | bytes 294920 | tf_op jit(solution)/shard_map/ppermute | solution.py:37
  120.2 3.0 %collective-permute-done.23.above_ref = bf16[96,512]{1,0:T(8,128)(2,1)S(1)} collective-permute-done((bf16[96,512]{1,0:T(8,128)(2,1)S(1)}, bf16[96,512]{1,0:T(8,128)(2,1)S(1)}, u32[]{:S(2)}, u32[]{:S(2)}) %collective-permute-start.23) | collective-permute-done | bytes 98336 | tf_op jit(solution)/shard_map/ppermute | solution.py:37
  124.2 4.5 %collective-permute-start.25 = (bf16[64,512]{1,0:T(8,128)(2,1)S(1)}, bf16[64,512]{1,0:T(8,128)(2,1)S(1)}, u32[]{:S(2)}, u32[]{:S(2)}) collective-permute-start(bf16[64,512]{1,0:T(8,128)(2,1)S(1)} %get-tuple-element.57), channel_id=1, source_target_pairs={{0,28},{4,0},{8,4},{12,8},{16,12},{20,16},{24,20},{28,24},{1,29},{... | collective-permute-start | bytes 196616 | tf_op jit(solution)/shard_map/ppermute | solution.py:37
  130.3 1.9 %collective-permute-start.27 = (bf16[192,512]{1,0:T(8,128)(2,1)S(1)}, bf16[192,512]{1,0:T(8,128)(2,1)S(1)}, u32[]{:S(2)}, u32[]{:S(2)}) collective-permute-start(bf16[192,512]{1,0:T(8,128)(2,1)S(1)} %constant_dynamic-update-slice_fusion.3.rims_ref), channel_id=1, source_target_pairs={{0,3},{1,0},{2,1},{3,2},{4,7},{5,4},{6,5},{7,6},{8,11},{9,8},{10,9... | collective-permute-start | bytes 589832 | tf_op jit(solution)/shard_map/ppermute | solution.py:37
  133.1 5.3 %collective-permute-done.27.above_ref = bf16[192,512]{1,0:T(8,128)(2,1)S(1)} collective-permute-done((bf16[192,512]{1,0:T(8,128)(2,1)S(1)}, bf16[192,512]{1,0:T(8,128)(2,1)S(1)}, u32[]{:S(2)}, u32[]{:S(2)}) %collective-permute-start.27) | collective-permute-done | bytes 196640 | tf_op jit(solution)/shard_map/ppermute | solution.py:37
  138.4 3.0 %lifted.3 = bf16[1024,512]{1,0:T(8,128)(2,1)} custom-call(bf16[256,512]{1,0:T(8,128)(2,1)S(1)} %get-tuple-element.56.coarse_ref, bf16[192,512]{1,0:T(8,128)(2,1)S(1)} %constant_dynamic-update-slice_fusion.3.rims_ref, bf16[192,512]{1,0:T(8,128)(2,1)S(1)} %collective-permute-done.26.below_ref, bf16[192,512]{1,0:T(8,128)(2,1)S(1)} %collective-permute-done.27.above_ref, ...), custom_call_target="tpu_custom_call" | custom-call | tf_op jit(solution)/shard_map/lifted/pallas_call | solution.py:414
  (105 shorter events, 18.3 us)
Async XLA Ops:
  1.6 16.2 %collective-permute-start.1 = (bf16[128,512]{1,0:T(8,128)(2,1)S(1)}, bf16[128,512]{1,0:T(8,128)(2,1)S(1)}, u32[]{:S(2)}, u32[]{:S(2)}) collective-permute-start(bf16[128,512]{1,0:T(8,128)(2,1)S(1)} %convolution_convert_fusion), channel_id=1, source_target_pairs={{0,28},{4,0},{8,4},{12,8},{16,12},{20,16},{24,20},{28,24},{1,29},{... | collective-permute-start | bytes 393224 | tf_op jit(solution)/shard_map/ppermute | solution.py:37
  6.8 11.1 %collective-permute-start = (bf16[128,512]{1,0:T(8,128)(2,1)S(1)}, bf16[128,512]{1,0:T(8,128)(2,1)S(1)}, u32[]{:S(2)}, u32[]{:S(2)}) collective-permute-start(bf16[128,512]{1,0:T(8,128)(2,1)S(1)} %convolution_convert_fusion), channel_id=1, source_target_pairs={{0,4},{4,8},{8,12},{12,16},{16,20},{20,24},{24,28},{28,0},{1,5},{5... | collective-permute-start | bytes 393224 | tf_op jit(solution)/shard_map/ppermute | solution.py:37
  17.9 13.4 %collective-permute-start.3 = (bf16[384,512]{1,0:T(8,128)(2,1)S(1)}, bf16[384,512]{1,0:T(8,128)(2,1)S(1)}, u32[]{:S(2)}, u32[]{:S(2)}) collective-permute-start(bf16[384,512]{1,0:T(8,128)(2,1)S(1)} %pad_maximum_fusion), channel_id=1, source_target_pairs={{0,3},{1,0},{2,1},{3,2},{4,7},{5,4},{6,5},{7,6},{8,11},{9,8},{10,9... | collective-permute-start | bytes 1179656 | tf_op jit(solution)/shard_map/ppermute | solution.py:37
  18.9 12.3 %collective-permute-start.2 = (bf16[384,512]{1,0:T(8,128)(2,1)S(1)}, bf16[384,512]{1,0:T(8,128)(2,1)S(1)}, u32[]{:S(2)}, u32[]{:S(2)}) collective-permute-start(bf16[384,512]{1,0:T(8,128)(2,1)S(1)} %pad_maximum_fusion), channel_id=1, source_target_pairs={{0,1},{1,2},{2,3},{3,0},{4,5},{5,6},{6,7},{7,4},{8,9},{9,10},{10,1... | collective-permute-start | bytes 1179656 | tf_op jit(solution)/shard_map/ppermute | solution.py:37
  57.6 5.6 %collective-permute-start.5 = (bf16[192,512]{1,0:T(8,128)(2,1)S(1)}, bf16[192,512]{1,0:T(8,128)(2,1)S(1)}, u32[]{:S(2)}, u32[]{:S(2)}) collective-permute-start(bf16[192,512]{1,0:T(8,128)(2,1)S(1)} %get-tuple-element.40), channel_id=1, source_target_pairs={{0,3},{1,0},{2,1},{3,2},{4,7},{5,4},{6,5},{7,6},{8,11},{9,8},{10,9... | collective-permute-start | bytes 589832 | tf_op jit(solution)/shard_map/ppermute | solution.py:37
  63.2 10.4 %collective-permute-start.6 = (bf16[128,512]{1,0:T(8,128)(2,1)S(1)}, bf16[128,512]{1,0:T(8,128)(2,1)S(1)}, u32[]{:S(2)}, u32[]{:S(2)}) collective-permute-start(bf16[128,512]{1,0:T(8,128)(2,1)S(1)} %get-tuple-element.41.right_ref), channel_id=1, source_target_pairs={{0,4},{4,8},{8,12},{12,16},{16,20},{20,24},{24,28},{28,0},{1,5},{5... | collective-permute-start | bytes 393224 | tf_op jit(solution)/shard_map/ppermute | solution.py:37
  63.3 10.3 %collective-permute-start.7 = (bf16[128,512]{1,0:T(8,128)(2,1)S(1)}, bf16[128,512]{1,0:T(8,128)(2,1)S(1)}, u32[]{:S(2)}, u32[]{:S(2)}) collective-permute-start(bf16[128,512]{1,0:T(8,128)(2,1)S(1)} %get-tuple-element.42.left_ref), channel_id=1, source_target_pairs={{0,28},{4,0},{8,4},{12,8},{16,12},{20,16},{24,20},{28,24},{1,29},{... | collective-permute-start | bytes 393224 | tf_op jit(solution)/shard_map/ppermute | solution.py:37
  67.6 5.5 %collective-permute-start.8 = (bf16[64,512]{1,0:T(8,128)(2,1)S(1)}, bf16[64,512]{1,0:T(8,128)(2,1)S(1)}, u32[]{:S(2)}, u32[]{:S(2)}) collective-permute-start(bf16[64,512]{1,0:T(8,128)(2,1)S(1)} %get-tuple-element.43), channel_id=1, source_target_pairs={{0,8},{4,12},{8,16},{12,20},{16,24},{20,28},{24,0},{28,4},{1,9},{5... | collective-permute-start | bytes 196616 | tf_op jit(solution)/shard_map/ppermute | solution.py:37
  67.6 6.0 %collective-permute-start.9 = (bf16[64,512]{1,0:T(8,128)(2,1)S(1)}, bf16[64,512]{1,0:T(8,128)(2,1)S(1)}, u32[]{:S(2)}, u32[]{:S(2)}) collective-permute-start(bf16[64,512]{1,0:T(8,128)(2,1)S(1)} %get-tuple-element.44), channel_id=1, source_target_pairs={{0,24},{4,28},{8,0},{12,4},{16,8},{20,12},{24,16},{28,20},{1,25},{... | collective-permute-start | bytes 196616 | tf_op jit(solution)/shard_map/ppermute | solution.py:37
  73.7 7.4 %collective-permute-start.11 = (bf16[192,512]{1,0:T(8,128)(2,1)S(1)}, bf16[192,512]{1,0:T(8,128)(2,1)S(1)}, u32[]{:S(2)}, u32[]{:S(2)}) collective-permute-start(bf16[192,512]{1,0:T(8,128)(2,1)S(1)} %rim_sums.2.rims_ref), channel_id=1, source_target_pairs={{0,3},{1,0},{2,1},{3,2},{4,7},{5,4},{6,5},{7,6},{8,11},{9,8},{10,9... | collective-permute-start | bytes 589832 | tf_op jit(solution)/shard_map/ppermute | solution.py:37
  74.5 6.6 %collective-permute-start.10 = (bf16[192,512]{1,0:T(8,128)(2,1)S(1)}, bf16[192,512]{1,0:T(8,128)(2,1)S(1)}, u32[]{:S(2)}, u32[]{:S(2)}) collective-permute-start(bf16[192,512]{1,0:T(8,128)(2,1)S(1)} %rim_sums.2.rims_ref), channel_id=1, source_target_pairs={{0,1},{1,2},{2,3},{3,0},{4,5},{5,6},{6,7},{7,4},{8,9},{9,10},{10,1... | collective-permute-start | bytes 589832 | tf_op jit(solution)/shard_map/ppermute | solution.py:37
  94.5 9.3 %collective-permute-start.14 = (bf16[64,512]{1,0:T(8,128)(2,1)S(1)}, bf16[64,512]{1,0:T(8,128)(2,1)S(1)}, u32[]{:S(2)}, u32[]{:S(2)}) collective-permute-start(bf16[64,512]{1,0:T(8,128)(2,1)S(1)} %get-tuple-element.49.right_ref), channel_id=1, source_target_pairs={{0,4},{4,8},{8,12},{12,16},{16,20},{20,24},{24,28},{28,0},{1,5},{5... | collective-permute-start | bytes 196616 | tf_op jit(solution)/shard_map/ppermute | solution.py:37
  94.6 9.3 %collective-permute-start.15 = (bf16[64,512]{1,0:T(8,128)(2,1)S(1)}, bf16[64,512]{1,0:T(8,128)(2,1)S(1)}, u32[]{:S(2)}, u32[]{:S(2)}) collective-permute-start(bf16[64,512]{1,0:T(8,128)(2,1)S(1)} %get-tuple-element.50.left_ref), channel_id=1, source_target_pairs={{0,28},{4,0},{8,4},{12,8},{16,12},{20,16},{24,20},{28,24},{1,29},{... | collective-permute-start | bytes 196616 | tf_op jit(solution)/shard_map/ppermute | solution.py:37
  98.7 5.1 %collective-permute-start.16 = (bf16[32,512]{1,0:T(8,128)(2,1)S(1)}, bf16[32,512]{1,0:T(8,128)(2,1)S(1)}, u32[]{:S(2)}, u32[]{:S(2)}) collective-permute-start(bf16[32,512]{1,0:T(8,128)(2,1)S(1)} %get-tuple-element.51), channel_id=1, source_target_pairs={{0,8},{4,12},{8,16},{12,20},{16,24},{20,28},{24,0},{28,4},{1,9},{5... | collective-permute-start | bytes 98312 | tf_op jit(solution)/shard_map/ppermute | solution.py:37
  98.7 5.1 %collective-permute-start.17 = (bf16[32,512]{1,0:T(8,128)(2,1)S(1)}, bf16[32,512]{1,0:T(8,128)(2,1)S(1)}, u32[]{:S(2)}, u32[]{:S(2)}) collective-permute-start(bf16[32,512]{1,0:T(8,128)(2,1)S(1)} %get-tuple-element.52), channel_id=1, source_target_pairs={{0,24},{4,28},{8,0},{12,4},{16,8},{20,12},{24,16},{28,20},{1,25},{... | collective-permute-start | bytes 98312 | tf_op jit(solution)/shard_map/ppermute | solution.py:37
  103.9 5.1 %collective-permute-start.19 = (bf16[96,512]{1,0:T(8,128)(2,1)S(1)}, bf16[96,512]{1,0:T(8,128)(2,1)S(1)}, u32[]{:S(2)}, u32[]{:S(2)}) collective-permute-start(bf16[96,512]{1,0:T(8,128)(2,1)S(1)} %rim_sums.3.rims_ref), channel_id=1, source_target_pairs={{0,3},{1,0},{2,1},{3,2},{4,7},{5,4},{6,5},{7,6},{8,11},{9,8},{10,9... | collective-permute-start | bytes 294920 | tf_op jit(solution)/shard_map/ppermute | solution.py:37
  104.8 4.2 %collective-permute-start.18 = (bf16[96,512]{1,0:T(8,128)(2,1)S(1)}, bf16[96,512]{1,0:T(8,128)(2,1)S(1)}, u32[]{:S(2)}, u32[]{:S(2)}) collective-permute-start(bf16[96,512]{1,0:T(8,128)(2,1)S(1)} %rim_sums.3.rims_ref), channel_id=1, source_target_pairs={{0,1},{1,2},{2,3},{3,0},{4,5},{5,6},{6,7},{7,4},{8,9},{9,10},{10,1... | collective-permute-start | bytes 294920 | tf_op jit(solution)/shard_map/ppermute | solution.py:37
  112.2 5.5 %collective-permute-start.20 = (bf16[32,512]{1,0:T(8,128)(2,1)S(1)}, bf16[32,512]{1,0:T(8,128)(2,1)S(1)}, u32[]{:S(2)}, u32[]{:S(2)}) collective-permute-start(bf16[32,512]{1,0:T(8,128)(2,1)S(1)} %get-tuple-element.54), channel_id=1, source_target_pairs={{0,4},{4,8},{8,12},{12,16},{16,20},{20,24},{24,28},{28,0},{1,5},{5... | collective-permute-start | bytes 98312 | tf_op jit(solution)/shard_map/ppermute | solution.py:37
  112.3 5.5 %collective-permute-start.21 = (bf16[32,512]{1,0:T(8,128)(2,1)S(1)}, bf16[32,512]{1,0:T(8,128)(2,1)S(1)}, u32[]{:S(2)}, u32[]{:S(2)}) collective-permute-start(bf16[32,512]{1,0:T(8,128)(2,1)S(1)} %get-tuple-element.54), channel_id=1, source_target_pairs={{0,28},{4,0},{8,4},{12,8},{16,12},{20,16},{24,20},{28,24},{1,29},{... | collective-permute-start | bytes 98312 | tf_op jit(solution)/shard_map/ppermute | solution.py:37
  117.8 5.4 %collective-permute-start.23 = (bf16[96,512]{1,0:T(8,128)(2,1)S(1)}, bf16[96,512]{1,0:T(8,128)(2,1)S(1)}, u32[]{:S(2)}, u32[]{:S(2)}) collective-permute-start(bf16[96,512]{1,0:T(8,128)(2,1)S(1)} %constant_dynamic-update-slice_fusion.rims_ref), channel_id=1, source_target_pairs={{0,3},{1,0},{2,1},{3,2},{4,7},{5,4},{6,5},{7,6},{8,11},{9,8},{10,9... | collective-permute-start | bytes 294920 | tf_op jit(solution)/shard_map/ppermute | solution.py:37
  124.1 6.1 %collective-permute-start.24 = (bf16[64,512]{1,0:T(8,128)(2,1)S(1)}, bf16[64,512]{1,0:T(8,128)(2,1)S(1)}, u32[]{:S(2)}, u32[]{:S(2)}) collective-permute-start(bf16[64,512]{1,0:T(8,128)(2,1)S(1)} %get-tuple-element.57), channel_id=1, source_target_pairs={{0,4},{4,8},{8,12},{12,16},{16,20},{20,24},{24,28},{28,0},{1,5},{5... | collective-permute-start | bytes 196616 | tf_op jit(solution)/shard_map/ppermute | solution.py:37
  124.2 6.1 %collective-permute-start.25 = (bf16[64,512]{1,0:T(8,128)(2,1)S(1)}, bf16[64,512]{1,0:T(8,128)(2,1)S(1)}, u32[]{:S(2)}, u32[]{:S(2)}) collective-permute-start(bf16[64,512]{1,0:T(8,128)(2,1)S(1)} %get-tuple-element.57), channel_id=1, source_target_pairs={{0,28},{4,0},{8,4},{12,8},{16,12},{20,16},{24,20},{28,24},{1,29},{... | collective-permute-start | bytes 196616 | tf_op jit(solution)/shard_map/ppermute | solution.py:37
  130.3 8.1 %collective-permute-start.27 = (bf16[192,512]{1,0:T(8,128)(2,1)S(1)}, bf16[192,512]{1,0:T(8,128)(2,1)S(1)}, u32[]{:S(2)}, u32[]{:S(2)}) collective-permute-start(bf16[192,512]{1,0:T(8,128)(2,1)S(1)} %constant_dynamic-update-slice_fusion.3.rims_ref), channel_id=1, source_target_pairs={{0,3},{1,0},{2,1},{3,2},{4,7},{5,4},{6,5},{7,6},{8,11},{9,8},{10,9... | collective-permute-start | bytes 589832 | tf_op jit(solution)/shard_map/ppermute | solution.py:37
  132.3 6.1 %collective-permute-start.26 = (bf16[192,512]{1,0:T(8,128)(2,1)S(1)}, bf16[192,512]{1,0:T(8,128)(2,1)S(1)}, u32[]{:S(2)}, u32[]{:S(2)}) collective-permute-start(bf16[192,512]{1,0:T(8,128)(2,1)S(1)} %constant_dynamic-update-slice_fusion.3.rims_ref), channel_id=1, source_target_pairs={{0,1},{1,2},{2,3},{3,0},{4,5},{5,6},{6,7},{7,4},{8,9},{9,10},{10,1... | collective-permute-start | bytes 589832 | tf_op jit(solution)/shard_map/ppermute | solution.py:37
  (27 other events, 740.3 us)

commit v3 on v2

--- a/solution.py
+++ b/solution.py
@@ -11,7 +11,8 @@
 CB2 = 32
 LANES = 128
 VMEM_BYTES = 40 * 1024 * 1024
-PART_DTYPE = jnp.float32
+PART_DTYPE = jnp.bfloat16
+ROWS = 512
 
 VSPEC = pl.BlockSpec(memory_space=pltpu.VMEM)
 SSPEC = pl.BlockSpec(memory_space=pltpu.SMEM)
@@ -27,7 +28,7 @@
 
 def params(grid=False):
     return pltpu.CompilerParams(
-        dimension_semantics=("arbitrary",) if grid else None, vmem_limit_bytes=VMEM_BYTES
+        dimension_semantics=("arbitrary",) if grid else None, vmem_limit_bytes=VMEM_BYTES,
     )
 
 
@@ -67,11 +68,6 @@
 
 def line(table, row, C):
     return table[pl.ds(pl.multiple_of(row * C, C), C), :]
-
-
-def spread(lines, reads, C):
-    for j, read in enumerate(reads):
-        lines[C * j : C * (j + 1), :] = read()
 
 
 def onehot_sum(targets, messages, first, count):
@@ -114,58 +110,53 @@
     ]
 
 
-def edge_start(dst, nodes_in, latent, message_in, block, begin, blocks, part=None):
+def edge_start(dst, nodes_in, latent, message_in, block, begin, blocks, part=None, table_in=None):
     nodes, features = nodes_in.shape
     edges = latent.shape[0]
     C = features // LANES
     opening = part is None
 
-    def kernel(dst_ref, node_ref, latent_ref, in_ref, *rest):
-        part_ref = rest[0 if opening else 1]
-        table, lines0, lines1 = rest[-3:]
+    def kernel(dst_ref, latent_ref, last_ref, first_in, second_in, *rest):
+        if opening:
+            third_in, part_ref, source_ref, table = rest[:4]
+        else:
+            table, part_ref = first_in, rest[0]
+        lines0, lines1 = rest[-2:]
         step = pl.program_id(0)
-
-        def gather(at, lines):
-            base = (begin + jnp.minimum(at, blocks - 1)) * block
-            spread(lines, [lambda j=j: line(table, dst_ref[base + j], C) for j in range(block)], C)
-
-        def project(half, lines):
-            rows = slice(half * block, (half + 1) * block)
-            part_ref[rows, :] = (
-                dotf(latent_ref[rows, :], in_ref[2 * features :, :]) + get_rows(lines, 0, block, C)
-            ).astype(part_ref.dtype)
 
         @pl.when(step == 0)
         def _():
-            put_rows(table, 0, dotf(node_ref[...], in_ref[features : 2 * features, :]))
             if opening:
-                put_rows(rest[1], 0, dotf(node_ref[...], in_ref[:features, :]))
-            gather(0, lines0)
-
-        gather(2 * step + 1, lines1)
-        project(0, lines0)
-        gather(2 * step + 2, lines0)
-        project(1, lines1)
+                put_rows(table, 0, dotf(first_in[...], third_in[...]))
+                put_rows(source_ref, 0, dotf(first_in[...], second_in[...]))
+
+        base = (begin + 2 * step) * block
+        for half, lines in ((0, lines0), (1, lines1)):
+            rows = slice(half * block, (half + 1) * block)
+            value = dotf(latent_ref[rows, :], last_ref[...])
+            for j in range(block):
+                lines[C * j : C * (j + 1), :] = line(table, dst_ref[base + half * block + j], C)
+            part_ref[rows, :] = (value + get_rows(lines, 0, block, C)).astype(part_ref.dtype)
 
     start = begin // 2
     tile = pl.BlockSpec((2 * block, features), lambda i, *_: (i + start, 0))
+    weights = [pl.BlockSpec((features, features), lambda i, *_, p=p: (p, 0)) for p in range(3)]
     part_shape = jax.ShapeDtypeStruct((edges, features), PART_DTYPE)
+    lines_shape = jax.ShapeDtypeStruct((nodes * C, LANES), jnp.float32)
+    if opening:
+        more, specs = [in_hbm(nodes_in)] + [in_hbm(message_in)] * 2, [whole(nodes, features)] + weights[:2]
+    else:
+        more, specs = [table_in, in_hbm(part)], [VSPEC, pl.BlockSpec(memory_space=pl.ANY)]
     return pl.pallas_call(
         kernel,
         grid_spec=pltpu.PrefetchScalarGridSpec(
             num_scalar_prefetch=1,
             grid=(blocks // 2,),
-            in_specs=[whole(nodes, features), tile, whole(3 * features, features)] + ([] if opening else [pl.BlockSpec(memory_space=pl.ANY)]),
-            out_specs=[tile, VSPEC] if opening else tile,
-            scratch_shapes=[
-                pltpu.VMEM((nodes * C, LANES), jnp.float32),
-                pltpu.VMEM((block * C, LANES), jnp.float32),
-                pltpu.VMEM((block * C, LANES), jnp.float32),
-            ],
+            in_specs=[tile, weights[2]] + specs,
+            out_specs=[tile, VSPEC, VSPEC] if opening else tile,
+            scratch_shapes=[pltpu.VMEM((block * C, LANES), jnp.float32)] * 2,
         ),
-        out_shape=[part_shape, jax.ShapeDtypeStruct((nodes * C, LANES), jnp.float32)]
-        if opening
-        else part_shape,
+        out_shape=[part_shape, lines_shape, lines_shape] if opening else part_shape,
         input_output_aliases={} if opening else {4: 0},
         compiler_params=params(True),
         cost_estimate=pl.CostEstimate(
@@ -173,7 +164,7 @@
             bytes_accessed=6 * blocks * block * features,
         ),
         name="edge_start",
-    )(in_hbm(dst), in_hbm(nodes_in), in_hbm(latent), in_hbm(message_in), *(() if opening else (in_hbm(part),)))
+    )(in_hbm(dst), in_hbm(latent), in_hbm(message_in), *more)
 
 
 def fine_stage(src, dst, nodes_in, own_lines, left, right, below, above, part, parents, weights,
@@ -189,8 +180,9 @@
                ugain_ref, new_ref, sums_ref, up_ref, mid_ref, down_ref, table, lines0, lines1, acc, sent):
         step = pl.program_id(0)
 
-        def gather(base, lines):
-            spread(lines, [lambda j=j: line(table, src_ref[base + j], C) for j in range(block)], C)
+        def gather(base, lines, first, count):
+            for j in range(first, first + count):
+                lines[C * j : C * (j + 1), :] = line(table, src_ref[base + j], C)
 
         @pl.when(step == 0)
         def _():
@@ -203,7 +195,8 @@
             put_rows(table, nodes + rim, dotf(left_ref[...], first))
             put_rows(table, nodes + 7 * rim, dotf(right_ref[...], first))
             acc[...] = jnp.zeros_like(acc)
-            gather(0, lines0)
+            gather(0, lines0, 0, block)
+            gather(block, lines1, 0, block)
 
         def block_sum(half, lines):
             preact = part_ref[half * block : (half + 1) * block, :].astype(jnp.float32) + get_rows(lines, 0, block, C)
@@ -211,12 +204,15 @@
             messages = normed(dotf(hidden, out_ref[...]), gain_ref[...].astype(jnp.float32))
             sent[half * block : (half + 1) * block, :] = messages.astype(jnp.bfloat16)
 
-        gather((2 * step + 1) * block, lines1)
         block_sum(0, lines0)
-        gather(jnp.minimum(2 * step + 2, 2 * steps - 1) * block, lines0)
         block_sum(1, lines1)
-        for n in range(0, nodes, 256):
-            acc[n : n + 256, :] += onehot_sum(dst_ref[...], sent[...], n, 256)
+        later = jnp.minimum(step + 1, steps - 1) * 2 * block
+        pieces = nodes // ROWS
+        for t in range(pieces):
+            lines, base = (lines0, later) if 2 * t < pieces else (lines1, later + block)
+            span = 2 * block // pieces
+            gather(base, lines, (t * span) % block, span)
+            acc[t * ROWS : (t + 1) * ROWS, :] += onehot_sum(dst_ref[...], sent[...], t * ROWS, ROWS)
 
         @pl.when(step == steps - 1)
         def _():
@@ -462,16 +458,19 @@
     nodes, features = fine_nodes.shape
     pick = (boundary[:, None] == lax.iota(jnp.int32, nodes)[None, :]).astype(jnp.bfloat16)
     edge_rows = dotf(pick, fine_nodes).astype(jnp.bfloat16)
-    half = edge_latent.shape[0] // 1024
+    blocks = edge_latent.shape[0] // 512
+    early = blocks // 3 // 2 * 2
     left = passed_along(edge_rows, "gx", 1)
     right = passed_along(edge_rows, "gx", -1)
-    part, own_lines = edge_start(fine_dst, fine_nodes, edge_latent, fine_message_in, 512, 0, half)
+    part, own_lines, targets = edge_start(
+        fine_dst, fine_nodes, edge_latent, fine_message_in, 512, 0, early
+    )
     left, right, part = lax.optimization_barrier((left, right, part))
     stack = jnp.concatenate([left, edge_rows, right], axis=0)
     below = passed_along(stack, "gy", 1)
     above = passed_along(stack, "gy", -1)
     part = edge_start(
-        fine_dst, fine_nodes, edge_latent, fine_message_in, 512, half, half, part
+        fine_dst, fine_nodes, edge_latent, fine_message_in, 512, early, blocks - early, part, targets
     )
     fine_new, sums, up, mid, down = fine_stage(
         fine_src, fine_dst, fine_nodes, own_lines, left, right, below, above, part,

time: 142 us -> 137 us (0.965)
  Pallas kernels: 62.7 us -> 54.5 us
  local copies, waits for them, and re-layouts: 0.2 us -> 2.88 us
    pallas_call x2, Pallas kernels: 21.9 us -> 17.4 us  [edge_start(): pl.pallas_call(kernel, grid_spec=pltpu.PrefetchScalarGridSpec(num_scalar_...]
    pallas_call x1, Pallas kernels: 25.7 us -> 22 us  [fine_stage(): pl.pallas_call(kernel, grid_spec=pltpu.PrefetchScalarGridSpec(num_scalar_...]
    unnamed x50 -> x52, local copies, waits for them, and re-layouts: 0.15 us -> 2.84 us
  transfers between devices with their start and end apart: 28 -> 28, of which waited for: 13 -> 14; matrix products, arithmetic and copies ran while one was open for 0% -> 0% of each run, Pallas kernels for 16% -> 13%
where the time goes in v3:
time: 137 us; the launch traced here: 136 us
  Pallas kernels  54.5 us (40%)
  starting transfers between devices  42.8 us (31%)
  waiting for transfers between devices  33.4 us (24%)
  local copies, waits for them, and re-layouts  2.88 us (2%)
  matrix products  1.59 us (1%)
    ppermute x28, starting transfers between devices, passed_along(): return lax.ppermute(value, axis, pairs)  42.8 us
    ppermute x28, waiting for transfers between devices, passed_along(): return lax.ppermute(value, axis, pairs)  33.4 us
    pallas_call x1, Pallas kernels, fine_stage(): pl.pallas_call(kernel, grid_spec=pltpu.PrefetchScalarGridSpec(num_scalar_...  22 us
    pallas_call x2, Pallas kernels, edge_start(): pl.pallas_call(kernel, grid_spec=pltpu.PrefetchScalarGridSpec(num_scalar_...  17.4 us
    pallas_call x2, Pallas kernels, level_pass(): pl.pallas_call(kernel, in_specs=[VSPEC] * 4 + [SSPEC] * 2 + [VSPEC] * 9,...  11 us
    pallas_call x2, Pallas kernels, lifted(): pl.pallas_call(kernel, in_specs=[VSPEC] * 4 + [SSPEC, VSPEC], out_specs=[...  3.9 us
    unnamed x52, local copies, waits for them, and re-layouts  2.84 us
  transfers between devices with their start and end apart: 28, of which 14 were waited for; matrix products, arithmetic and copies ran while one was open for 0% of the time, Pallas kernels for 13%

profile of v3, /device:TPU:1, one launch (start us, length us, event | category | flops | bytes accessed | tf_op | source)
XLA Modules:
  0.0 135.7 jit_solution(11863789144919962009)
XLA Ops:
  1.6 5.1 %collective-permute-start.1 = (bf16[128,512]{1,0:T(8,128)(2,1)S(1)}, bf16[128,512]{1,0:T(8,128)(2,1)S(1)}, u32[]{:S(2)}, u32[]{:S(2)}) collective-permute-start(bf16[128,512]{1,0:T(8,128)(2,1)S(1)} %convolution_convert_fusion), channel_id=1, source_target_pairs={{0,28},{4,0},{8,4},{12,8},{16,12},{20,16},{24,20},{28,24},{1,29},{... | collective-permute-start | bytes 393224 | tf_op jit(solution)/shard_map/ppermute | solution.py:38
  6.8 7.4 %edge_start.2 = (bf16[6144,512]{1,0:T(8,128)(2,1)S(1)}, f32[4096,128]{1,0:T(8,128)S(1)}, f32[4096,128]{1,0:T(8,128)S(1)}) custom-call(s32[6144]{0:T(1024)} %dst_ref.5, bf16[6144,512]{1,0:T(8,128)(2,1)} %latent_ref.3, bf16[1536,512]{1,0:T(8,128)(2,1)} %in_ref.3, bf16[1024,512]{1,0:T(8,128)(2,1)} %node_ref.1, bf16[1536,512]{1,0:T(8,128)(2,1)} %in_ref.3, ...), custom_call_target="tpu_custom_call" | custom-call | flops 1073741824 | bytes 6291456 | tf_op jit(solution)/shard_map/edge_start/pallas_call | solution.py:150
  14.2 2.7 %copy-done.1 = bf16[6144,512]{1,0:T(8,128)(2,1)} copy-done((bf16[6144,512]{1,0:T(8,128)(2,1)}, bf16[6144,512]{1,0:T(8,128)(2,1)S(1)}, u32[]{:S(2)}) %copy-start.1) | copy-done | bytes 6291480
  19.2 10.0 %edge_start.3.part_ref = bf16[6144,512]{1,0:T(8,128)(2,1)} custom-call(s32[6144]{0:T(1024)} %dst_ref.5, bf16[6144,512]{1,0:T(8,128)(2,1)} %latent_ref.3, bf16[1536,512]{1,0:T(8,128)(2,1)} %in_ref.3, f32[4096,128]{1,0:T(8,128)S(1)} %get-tuple-element.37.first_in, bf16[6144,512]{1,0:T(8,128)(2,1)} %copy-done.1), custom_call_target="tpu_custom_call", output_to_operand_aliasing={{}: (4, {})} | custom-call | flops 2147483648 | bytes 12582912 | tf_op jit(solution)/shard_map/edge_start/pallas_call | solution.py:150
  29.4 22.0 %fine_stage.1 = (bf16[1024,512]{1,0:T(8,128)(2,1)S(1)}, f32[256,512]{1,0:T(8,128)S(1)}, bf16[192,512]{1,0:T(8,128)(2,1)S(1)}, f32[192,512]{1,0:T(8,128)S(1)}, bf16[192,512]{1,0:T(8,128)(2,1)S(1)}) custom-call(s32[6144]{0:T(1024)S(1)} %copy-done.12, bf16[1024,512]{1,0:T(8,128)(2,1)S(1)} %copy-done.2, f32[4096,128]{1,0:T(8,128)S(1)} %get-tuple-element.33.own_ref, ...), custom_call_target="tpu_custom_call" | custom-call | tf_op jit(solution)/shard_map/fine_stage/pallas_call | solution.py:224
  52.5 3.6 %collective-permute-done.4.below_ref = bf16[192,512]{1,0:T(8,128)(2,1)S(1)} collective-permute-done((bf16[192,512]{1,0:T(8,128)(2,1)S(1)}, bf16[192,512]{1,0:T(8,128)(2,1)S(1)}, u32[]{:S(2)}, u32[]{:S(2)}) %collective-permute-start.4) | collective-permute-done | bytes 196640 | tf_op jit(solution)/shard_map/ppermute | solution.py:38
  56.1 2.1 %collective-permute-done.5.above_ref = bf16[192,512]{1,0:T(8,128)(2,1)S(1)} collective-permute-done((bf16[192,512]{1,0:T(8,128)(2,1)S(1)}, bf16[192,512]{1,0:T(8,128)(2,1)S(1)}, u32[]{:S(2)}, u32[]{:S(2)}) %collective-permute-start.5) | collective-permute-done | bytes 196640 | tf_op jit(solution)/shard_map/ppermute | solution.py:38
  58.3 4.5 %collective-permute-start.7 = (bf16[128,512]{1,0:T(8,128)(2,1)S(1)}, bf16[128,512]{1,0:T(8,128)(2,1)S(1)}, u32[]{:S(2)}, u32[]{:S(2)}) collective-permute-start(bf16[128,512]{1,0:T(8,128)(2,1)S(1)} %get-tuple-element.44.left_ref), channel_id=1, source_target_pairs={{0,28},{4,0},{8,4},{12,8},{16,12},{20,16},{24,20},{28,24},{1,29},{... | collective-permute-start | bytes 393224 | tf_op jit(solution)/shard_map/ppermute | solution.py:38
  62.8 3.3 %collective-permute-start.9 = (bf16[64,512]{1,0:T(8,128)(2,1)S(1)}, bf16[64,512]{1,0:T(8,128)(2,1)S(1)}, u32[]{:S(2)}, u32[]{:S(2)}) collective-permute-start(bf16[64,512]{1,0:T(8,128)(2,1)S(1)} %get-tuple-element.46), channel_id=1, source_target_pairs={{0,24},{4,28},{8,0},{12,4},{16,8},{20,12},{24,16},{28,20},{1,25},{... | collective-permute-start | bytes 196616 | tf_op jit(solution)/shard_map/ppermute | solution.py:38
  66.1 2.4 %collective-permute-done.8.a2 = bf16[64,512]{1,0:T(8,128)(2,1)S(1)} collective-permute-done((bf16[64,512]{1,0:T(8,128)(2,1)S(1)}, bf16[64,512]{1,0:T(8,128)(2,1)S(1)}, u32[]{:S(2)}, u32[]{:S(2)}) %collective-permute-start.8) | collective-permute-done | bytes 65568 | tf_op jit(solution)/shard_map/ppermute | solution.py:38
  70.9 5.6 %collective-permute-done.11.above_ref = bf16[192,512]{1,0:T(8,128)(2,1)S(1)} collective-permute-done((bf16[192,512]{1,0:T(8,128)(2,1)S(1)}, bf16[192,512]{1,0:T(8,128)(2,1)S(1)}, u32[]{:S(2)}, u32[]{:S(2)}) %collective-permute-start.11) | collective-permute-done | bytes 196640 | tf_op jit(solution)/shard_map/ppermute | solution.py:38
  76.5 7.8 %level_pass.2 = (bf16[256,512]{1,0:T(8,128)(2,1)S(1)}, f32[64,512]{1,0:T(8,128)S(1)}, bf16[96,512]{1,0:T(8,128)(2,1)S(1)}, f32[96,512]{1,0:T(8,128)S(1)}, bf16[96,512]{1,0:T(8,128)(2,1)S(1)}) custom-call(f32[256,512]{1,0:T(8,128)S(1)} %get-tuple-element.39.sums_ref, bf16[192,512]{1,0:T(8,128)(2,1)S(1)} %rim_sums.2.rims_ref, ...), custom_call_target="tpu_custom_call" | custom-call | tf_op jit(solution)/shard_map/level_pass/pallas_call | solution.py:365
  86.8 2.5 %collective-permute-done.13.above_ref = bf16[96,512]{1,0:T(8,128)(2,1)S(1)} collective-permute-done((bf16[96,512]{1,0:T(8,128)(2,1)S(1)}, bf16[96,512]{1,0:T(8,128)(2,1)S(1)}, u32[]{:S(2)}, u32[]{:S(2)}) %collective-permute-start.13) | collective-permute-done | bytes 98336 | tf_op jit(solution)/shard_map/ppermute | solution.py:38
  89.4 4.1 %collective-permute-start.15 = (bf16[64,512]{1,0:T(8,128)(2,1)S(1)}, bf16[64,512]{1,0:T(8,128)(2,1)S(1)}, u32[]{:S(2)}, u32[]{:S(2)}) collective-permute-start(bf16[64,512]{1,0:T(8,128)(2,1)S(1)} %get-tuple-element.52.left_ref), channel_id=1, source_target_pairs={{0,28},{4,0},{8,4},{12,8},{16,12},{20,16},{24,20},{28,24},{1,29},{... | collective-permute-start | bytes 196616 | tf_op jit(solution)/shard_map/ppermute | solution.py:38
  93.5 3.3 %collective-permute-start.17 = (bf16[32,512]{1,0:T(8,128)(2,1)S(1)}, bf16[32,512]{1,0:T(8,128)(2,1)S(1)}, u32[]{:S(2)}, u32[]{:S(2)}) collective-permute-start(bf16[32,512]{1,0:T(8,128)(2,1)S(1)} %get-tuple-element.54), channel_id=1, source_target_pairs={{0,24},{4,28},{8,0},{12,4},{16,8},{20,12},{24,16},{28,20},{1,25},{... | collective-permute-start | bytes 98312 | tf_op jit(solution)/shard_map/ppermute | solution.py:38
  100.3 2.2 %collective-permute-done.19.above_ref = bf16[96,512]{1,0:T(8,128)(2,1)S(1)} collective-permute-done((bf16[96,512]{1,0:T(8,128)(2,1)S(1)}, bf16[96,512]{1,0:T(8,128)(2,1)S(1)}, u32[]{:S(2)}, u32[]{:S(2)}) %collective-permute-start.19) | collective-permute-done | bytes 98336 | tf_op jit(solution)/shard_map/ppermute | solution.py:38
  102.6 3.2 %level_pass.3 = (bf16[64,512]{1,0:T(8,128)(2,1)S(1)}, bf16[32,512]{1,0:T(8,128)(2,1)S(1)}) custom-call(f32[64,512]{1,0:T(8,128)S(1)} %get-tuple-element.47.sums_ref, bf16[96,512]{1,0:T(8,128)(2,1)S(1)} %rim_sums.3.rims_ref, bf16[96,512]{1,0:T(8,128)(2,1)S(1)} %collective-permute-done.18.below_ref, bf16[96,512]{1,0:T(8,128)(2,1)S(1)} %collective-permute-done.19.above_ref, ...), custom_call_target="tpu_custom_call" | custom-call | tf_op jit(solution)/shard_map/level_pass/pallas_call | solution.py:365
  106.3 3.7 %collective-permute-start.21 = (bf16[32,512]{1,0:T(8,128)(2,1)S(1)}, bf16[32,512]{1,0:T(8,128)(2,1)S(1)}, u32[]{:S(2)}, u32[]{:S(2)}) collective-permute-start(bf16[32,512]{1,0:T(8,128)(2,1)S(1)} %get-tuple-element.56), channel_id=1, source_target_pairs={{0,28},{4,0},{8,4},{12,8},{16,12},{20,16},{24,20},{28,24},{1,29},{... | collective-permute-start | bytes 98312 | tf_op jit(solution)/shard_map/ppermute | solution.py:38
  111.4 2.9 %collective-permute-start.23 = (bf16[96,512]{1,0:T(8,128)(2,1)S(1)}, bf16[96,512]{1,0:T(8,128)(2,1)S(1)}, u32[]{:S(2)}, u32[]{:S(2)}) collective-permute-start(bf16[96,512]{1,0:T(8,128)(2,1)S(1)} %constant_dynamic-update-slice_fusion.rims_ref), channel_id=1, source_target_pairs={{0,3},{1,0},{2,1},{3,2},{4,7},{5,4},{6,5},{7,6},{8,11},{9,8},{10,9... | collective-permute-start | bytes 294920 | tf_op jit(solution)/shard_map/ppermute | solution.py:38
  115.1 3.2 %collective-permute-done.23.above_ref = bf16[96,512]{1,0:T(8,128)(2,1)S(1)} collective-permute-done((bf16[96,512]{1,0:T(8,128)(2,1)S(1)}, bf16[96,512]{1,0:T(8,128)(2,1)S(1)}, u32[]{:S(2)}, u32[]{:S(2)}) %collective-permute-start.23) | collective-permute-done | bytes 98336 | tf_op jit(solution)/shard_map/ppermute | solution.py:38
  119.4 4.5 %collective-permute-start.25 = (bf16[64,512]{1,0:T(8,128)(2,1)S(1)}, bf16[64,512]{1,0:T(8,128)(2,1)S(1)}, u32[]{:S(2)}, u32[]{:S(2)}) collective-permute-start(bf16[64,512]{1,0:T(8,128)(2,1)S(1)} %get-tuple-element.59), channel_id=1, source_target_pairs={{0,28},{4,0},{8,4},{12,8},{16,12},{20,16},{24,20},{28,24},{1,29},{... | collective-permute-start | bytes 196616 | tf_op jit(solution)/shard_map/ppermute | solution.py:38
  125.5 1.7 %collective-permute-start.27 = (bf16[192,512]{1,0:T(8,128)(2,1)S(1)}, bf16[192,512]{1,0:T(8,128)(2,1)S(1)}, u32[]{:S(2)}, u32[]{:S(2)}) collective-permute-start(bf16[192,512]{1,0:T(8,128)(2,1)S(1)} %constant_dynamic-update-slice_fusion.3.rims_ref), channel_id=1, source_target_pairs={{0,3},{1,0},{2,1},{3,2},{4,7},{5,4},{6,5},{7,6},{8,11},{9,8},{10,9... | collective-permute-start | bytes 589832 | tf_op jit(solution)/shard_map/ppermute | solution.py:38
  127.7 5.0 %collective-permute-done.27.above_ref = bf16[192,512]{1,0:T(8,128)(2,1)S(1)} collective-permute-done((bf16[192,512]{1,0:T(8,128)(2,1)S(1)}, bf16[192,512]{1,0:T(8,128)(2,1)S(1)}, u32[]{:S(2)}, u32[]{:S(2)}) %collective-permute-start.27) | collective-permute-done | bytes 196640 | tf_op jit(solution)/shard_map/ppermute | solution.py:38
  132.7 3.0 %lifted.3 = bf16[1024,512]{1,0:T(8,128)(2,1)} custom-call(bf16[256,512]{1,0:T(8,128)(2,1)S(1)} %get-tuple-element.58.coarse_ref, bf16[192,512]{1,0:T(8,128)(2,1)S(1)} %constant_dynamic-update-slice_fusion.3.rims_ref, bf16[192,512]{1,0:T(8,128)(2,1)S(1)} %collective-permute-done.26.below_ref, bf16[192,512]{1,0:T(8,128)(2,1)S(1)} %collective-permute-done.27.above_ref, ...), custom_call_target="tpu_custom_call" | custom-call | tf_op jit(solution)/shard_map/lifted/pallas_call | solution.py:410
  (107 shorter events, 19.3 us)
Async XLA Ops:
  1.6 15.3 %collective-permute-start.1 = (bf16[128,512]{1,0:T(8,128)(2,1)S(1)}, bf16[128,512]{1,0:T(8,128)(2,1)S(1)}, u32[]{:S(2)}, u32[]{:S(2)}) collective-permute-start(bf16[128,512]{1,0:T(8,128)(2,1)S(1)} %convolution_convert_fusion), channel_id=1, source_target_pairs={{0,28},{4,0},{8,4},{12,8},{16,12},{20,16},{24,20},{28,24},{1,29},{... | collective-permute-start | bytes 393224 | tf_op jit(solution)/shard_map/ppermute | solution.py:38
  6.8 10.1 %collective-permute-start = (bf16[128,512]{1,0:T(8,128)(2,1)S(1)}, bf16[128,512]{1,0:T(8,128)(2,1)S(1)}, u32[]{:S(2)}, u32[]{:S(2)}) collective-permute-start(bf16[128,512]{1,0:T(8,128)(2,1)S(1)} %convolution_convert_fusion), channel_id=1, source_target_pairs={{0,4},{4,8},{8,12},{12,16},{16,20},{20,24},{24,28},{28,0},{1,5},{5... | collective-permute-start | bytes 393224 | tf_op jit(solution)/shard_map/ppermute | solution.py:38
  16.9 12.3 %collective-permute-start.3 = (bf16[384,512]{1,0:T(8,128)(2,1)S(1)}, bf16[384,512]{1,0:T(8,128)(2,1)S(1)}, u32[]{:S(2)}, u32[]{:S(2)}) collective-permute-start(bf16[384,512]{1,0:T(8,128)(2,1)S(1)} %pad_maximum_fusion), channel_id=1, source_target_pairs={{0,3},{1,0},{2,1},{3,2},{4,7},{5,4},{6,5},{7,6},{8,11},{9,8},{10,9... | collective-permute-start | bytes 1179656 | tf_op jit(solution)/shard_map/ppermute | solution.py:38
  17.9 11.3 %collective-permute-start.2 = (bf16[384,512]{1,0:T(8,128)(2,1)S(1)}, bf16[384,512]{1,0:T(8,128)(2,1)S(1)}, u32[]{:S(2)}, u32[]{:S(2)}) collective-permute-start(bf16[384,512]{1,0:T(8,128)(2,1)S(1)} %pad_maximum_fusion), channel_id=1, source_target_pairs={{0,1},{1,2},{2,3},{3,0},{4,5},{5,6},{6,7},{7,4},{8,9},{9,10},{10,1... | collective-permute-start | bytes 1179656 | tf_op jit(solution)/shard_map/ppermute | solution.py:38
  51.5 4.6 %collective-permute-start.4 = (bf16[192,512]{1,0:T(8,128)(2,1)S(1)}, bf16[192,512]{1,0:T(8,128)(2,1)S(1)}, u32[]{:S(2)}, u32[]{:S(2)}) collective-permute-start(bf16[192,512]{1,0:T(8,128)(2,1)S(1)} %get-tuple-element.41), channel_id=1, source_target_pairs={{0,1},{1,2},{2,3},{3,0},{4,5},{5,6},{6,7},{7,4},{8,9},{9,10},{10,1... | collective-permute-start | bytes 589832 | tf_op jit(solution)/shard_map/ppermute | solution.py:38
  52.5 5.7 %collective-permute-start.5 = (bf16[192,512]{1,0:T(8,128)(2,1)S(1)}, bf16[192,512]{1,0:T(8,128)(2,1)S(1)}, u32[]{:S(2)}, u32[]{:S(2)}) collective-permute-start(bf16[192,512]{1,0:T(8,128)(2,1)S(1)} %get-tuple-element.42), channel_id=1, source_target_pairs={{0,3},{1,0},{2,1},{3,2},{4,7},{5,4},{6,5},{7,6},{8,11},{9,8},{10,9... | collective-permute-start | bytes 589832 | tf_op jit(solution)/shard_map/ppermute | solution.py:38
  58.2 10.7 %collective-permute-start.6 = (bf16[128,512]{1,0:T(8,128)(2,1)S(1)}, bf16[128,512]{1,0:T(8,128)(2,1)S(1)}, u32[]{:S(2)}, u32[]{:S(2)}) collective-permute-start(bf16[128,512]{1,0:T(8,128)(2,1)S(1)} %get-tuple-element.43.right_ref), channel_id=1, source_target_pairs={{0,4},{4,8},{8,12},{12,16},{16,20},{20,24},{24,28},{28,0},{1,5},{5... | collective-permute-start | bytes 393224 | tf_op jit(solution)/shard_map/ppermute | solution.py:38
  58.3 10.6 %collective-permute-start.7 = (bf16[128,512]{1,0:T(8,128)(2,1)S(1)}, bf16[128,512]{1,0:T(8,128)(2,1)S(1)}, u32[]{:S(2)}, u32[]{:S(2)}) collective-permute-start(bf16[128,512]{1,0:T(8,128)(2,1)S(1)} %get-tuple-element.44.left_ref), channel_id=1, source_target_pairs={{0,28},{4,0},{8,4},{12,8},{16,12},{20,16},{24,20},{28,24},{1,29},{... | collective-permute-start | bytes 393224 | tf_op jit(solution)/shard_map/ppermute | solution.py:38
  62.8 5.7 %collective-permute-start.8 = (bf16[64,512]{1,0:T(8,128)(2,1)S(1)}, bf16[64,512]{1,0:T(8,128)(2,1)S(1)}, u32[]{:S(2)}, u32[]{:S(2)}) collective-permute-start(bf16[64,512]{1,0:T(8,128)(2,1)S(1)} %get-tuple-element.45), channel_id=1, source_target_pairs={{0,8},{4,12},{8,16},{12,20},{16,24},{20,28},{24,0},{28,4},{1,9},{5... | collective-permute-start | bytes 196616 | tf_op jit(solution)/shard_map/ppermute | solution.py:38
  62.8 6.1 %collective-permute-start.9 = (bf16[64,512]{1,0:T(8,128)(2,1)S(1)}, bf16[64,512]{1,0:T(8,128)(2,1)S(1)}, u32[]{:S(2)}, u32[]{:S(2)}) collective-permute-start(bf16[64,512]{1,0:T(8,128)(2,1)S(1)} %get-tuple-element.46), channel_id=1, source_target_pairs={{0,24},{4,28},{8,0},{12,4},{16,8},{20,12},{24,16},{28,20},{1,25},{... | collective-permute-start | bytes 196616 | tf_op jit(solution)/shard_map/ppermute | solution.py:38
  69.0 7.4 %collective-permute-start.11 = (bf16[192,512]{1,0:T(8,128)(2,1)S(1)}, bf16[192,512]{1,0:T(8,128)(2,1)S(1)}, u32[]{:S(2)}, u32[]{:S(2)}) collective-permute-start(bf16[192,512]{1,0:T(8,128)(2,1)S(1)} %rim_sums.2.rims_ref), channel_id=1, source_target_pairs={{0,3},{1,0},{2,1},{3,2},{4,7},{5,4},{6,5},{7,6},{8,11},{9,8},{10,9... | collective-permute-start | bytes 589832 | tf_op jit(solution)/shard_map/ppermute | solution.py:38
  69.5 7.0 %collective-permute-start.10 = (bf16[192,512]{1,0:T(8,128)(2,1)S(1)}, bf16[192,512]{1,0:T(8,128)(2,1)S(1)}, u32[]{:S(2)}, u32[]{:S(2)}) collective-permute-start(bf16[192,512]{1,0:T(8,128)(2,1)S(1)} %rim_sums.2.rims_ref), channel_id=1, source_target_pairs={{0,1},{1,2},{2,3},{3,0},{4,5},{5,6},{6,7},{7,4},{8,9},{9,10},{10,1... | collective-permute-start | bytes 589832 | tf_op jit(solution)/shard_map/ppermute | solution.py:38
  85.1 4.1 %collective-permute-start.13 = (bf16[96,512]{1,0:T(8,128)(2,1)S(1)}, bf16[96,512]{1,0:T(8,128)(2,1)S(1)}, u32[]{:S(2)}, u32[]{:S(2)}) collective-permute-start(bf16[96,512]{1,0:T(8,128)(2,1)S(1)} %get-tuple-element.50), channel_id=1, source_target_pairs={{0,3},{1,0},{2,1},{3,2},{4,7},{5,4},{6,5},{7,6},{8,11},{9,8},{10,9... | collective-permute-start | bytes 294920 | tf_op jit(solution)/shard_map/ppermute | solution.py:38
  89.3 9.0 %collective-permute-start.14 = (bf16[64,512]{1,0:T(8,128)(2,1)S(1)}, bf16[64,512]{1,0:T(8,128)(2,1)S(1)}, u32[]{:S(2)}, u32[]{:S(2)}) collective-permute-start(bf16[64,512]{1,0:T(8,128)(2,1)S(1)} %get-tuple-element.51.right_ref), channel_id=1, source_target_pairs={{0,4},{4,8},{8,12},{12,16},{16,20},{20,24},{24,28},{28,0},{1,5},{5... | collective-permute-start | bytes 196616 | tf_op jit(solution)/shard_map/ppermute | solution.py:38
  89.4 9.0 %collective-permute-start.15 = (bf16[64,512]{1,0:T(8,128)(2,1)S(1)}, bf16[64,512]{1,0:T(8,128)(2,1)S(1)}, u32[]{:S(2)}, u32[]{:S(2)}) collective-permute-start(bf16[64,512]{1,0:T(8,128)(2,1)S(1)} %get-tuple-element.52.left_ref), channel_id=1, source_target_pairs={{0,28},{4,0},{8,4},{12,8},{16,12},{20,16},{24,20},{28,24},{1,29},{... | collective-permute-start | bytes 196616 | tf_op jit(solution)/shard_map/ppermute | solution.py:38
  93.5 4.8 %collective-permute-start.16 = (bf16[32,512]{1,0:T(8,128)(2,1)S(1)}, bf16[32,512]{1,0:T(8,128)(2,1)S(1)}, u32[]{:S(2)}, u32[]{:S(2)}) collective-permute-start(bf16[32,512]{1,0:T(8,128)(2,1)S(1)} %get-tuple-element.53), channel_id=1, source_target_pairs={{0,8},{4,12},{8,16},{12,20},{16,24},{20,28},{24,0},{28,4},{1,9},{5... | collective-permute-start | bytes 98312 | tf_op jit(solution)/shard_map/ppermute | solution.py:38
  93.5 4.8 %collective-permute-start.17 = (bf16[32,512]{1,0:T(8,128)(2,1)S(1)}, bf16[32,512]{1,0:T(8,128)(2,1)S(1)}, u32[]{:S(2)}, u32[]{:S(2)}) collective-permute-start(bf16[32,512]{1,0:T(8,128)(2,1)S(1)} %get-tuple-element.54), channel_id=1, source_target_pairs={{0,24},{4,28},{8,0},{12,4},{16,8},{20,12},{24,16},{28,20},{1,25},{... | collective-permute-start | bytes 98312 | tf_op jit(solution)/shard_map/ppermute | solution.py:38
  105.8 5.5 %collective-permute-start.20 = (bf16[32,512]{1,0:T(8,128)(2,1)S(1)}, bf16[32,512]{1,0:T(8,128)(2,1)S(1)}, u32[]{:S(2)}, u32[]{:S(2)}) collective-permute-start(bf16[32,512]{1,0:T(8,128)(2,1)S(1)} %get-tuple-element.56), channel_id=1, source_target_pairs={{0,4},{4,8},{8,12},{12,16},{16,20},{20,24},{24,28},{28,0},{1,5},{5... | collective-permute-start | bytes 98312 | tf_op jit(solution)/shard_map/ppermute | solution.py:38
  106.3 5.0 %collective-permute-start.21 = (bf16[32,512]{1,0:T(8,128)(2,1)S(1)}, bf16[32,512]{1,0:T(8,128)(2,1)S(1)}, u32[]{:S(2)}, u32[]{:S(2)}) collective-permute-start(bf16[32,512]{1,0:T(8,128)(2,1)S(1)} %get-tuple-element.56), channel_id=1, source_target_pairs={{0,28},{4,0},{8,4},{12,8},{16,12},{20,16},{24,20},{28,24},{1,29},{... | collective-permute-start | bytes 98312 | tf_op jit(solution)/shard_map/ppermute | solution.py:38
  111.4 7.0 %collective-permute-start.23 = (bf16[96,512]{1,0:T(8,128)(2,1)S(1)}, bf16[96,512]{1,0:T(8,128)(2,1)S(1)}, u32[]{:S(2)}, u32[]{:S(2)}) collective-permute-start(bf16[96,512]{1,0:T(8,128)(2,1)S(1)} %constant_dynamic-update-slice_fusion.rims_ref), channel_id=1, source_target_pairs={{0,3},{1,0},{2,1},{3,2},{4,7},{5,4},{6,5},{7,6},{8,11},{9,8},{10,9... | collective-permute-start | bytes 294920 | tf_op jit(solution)/shard_map/ppermute | solution.py:38
  119.3 6.1 %collective-permute-start.24 = (bf16[64,512]{1,0:T(8,128)(2,1)S(1)}, bf16[64,512]{1,0:T(8,128)(2,1)S(1)}, u32[]{:S(2)}, u32[]{:S(2)}) collective-permute-start(bf16[64,512]{1,0:T(8,128)(2,1)S(1)} %get-tuple-element.59), channel_id=1, source_target_pairs={{0,4},{4,8},{8,12},{12,16},{16,20},{20,24},{24,28},{28,0},{1,5},{5... | collective-permute-start | bytes 196616 | tf_op jit(solution)/shard_map/ppermute | solution.py:38
  119.4 6.1 %collective-permute-start.25 = (bf16[64,512]{1,0:T(8,128)(2,1)S(1)}, bf16[64,512]{1,0:T(8,128)(2,1)S(1)}, u32[]{:S(2)}, u32[]{:S(2)}) collective-permute-start(bf16[64,512]{1,0:T(8,128)(2,1)S(1)} %get-tuple-element.59), channel_id=1, source_target_pairs={{0,28},{4,0},{8,4},{12,8},{16,12},{20,16},{24,20},{28,24},{1,29},{... | collective-permute-start | bytes 196616 | tf_op jit(solution)/shard_map/ppermute | solution.py:38
  125.5 7.2 %collective-permute-start.27 = (bf16[192,512]{1,0:T(8,128)(2,1)S(1)}, bf16[192,512]{1,0:T(8,128)(2,1)S(1)}, u32[]{:S(2)}, u32[]{:S(2)}) collective-permute-start(bf16[192,512]{1,0:T(8,128)(2,1)S(1)} %constant_dynamic-update-slice_fusion.3.rims_ref), channel_id=1, source_target_pairs={{0,3},{1,0},{2,1},{3,2},{4,7},{5,4},{6,5},{7,6},{8,11},{9,8},{10,9... | collective-permute-start | bytes 589832 | tf_op jit(solution)/shard_map/ppermute | solution.py:38
  127.1 5.6 %collective-permute-start.26 = (bf16[192,512]{1,0:T(8,128)(2,1)S(1)}, bf16[192,512]{1,0:T(8,128)(2,1)S(1)}, u32[]{:S(2)}, u32[]{:S(2)}) collective-permute-start(bf16[192,512]{1,0:T(8,128)(2,1)S(1)} %constant_dynamic-update-slice_fusion.3.rims_ref), channel_id=1, source_target_pairs={{0,1},{1,2},{2,3},{3,0},{4,5},{5,6},{6,7},{7,4},{8,9},{9,10},{10,1... | collective-permute-start | bytes 589832 | tf_op jit(solution)/shard_map/ppermute | solution.py:38
  (28 other events, 697.8 us)
